TPU v7x, 256 devices: a whole 4x4x8 slice. The times are simulated.
256 devices in a mesh: dp: 64 (over z, y, core), mp: 4 (over x).
Axes of the slice: x: 4, y: 4, z: 8, core: 2. Of those that a mesh axis runs over, the one named last changes fastest.
Arguments:
- pixels: bfloat16 [1024, 256, 768], P('dp', 'mp'), may hold values from -6 to 6
- selection: int32 [1024], P('dp'), may hold values from 0 to 1, as said below
- destination: int32 [1024], P('dp'), may hold values from 0 to 63, as said below
- patch_weight: bfloat16 [768, 1024], replicated, may hold values from -0.21875 to 0.21875
- position: bfloat16 [256, 1024], P('mp'), may hold values from -6 to 6
- query_key_value: bfloat16 [3, 1024, 1024], P(None, None, 'mp'), may hold values from -1 to 1
- output_weight: bfloat16 [1024, 1024], P('mp'), may hold values from -0.1875 to 0.1875
- up_weight: bfloat16 [1024, 4096], P(None, 'mp'), may hold values from -0.1875 to 0.1875
- down_weight: bfloat16 [4096, 1024], P('mp'), may hold values from -0.09375 to 0.09375
- norm_gains: float32 [3, 1024], replicated, may hold values from 0.25 to 1.75
- embedding_weight: bfloat16 [1024, 1024], replicated, may hold values from -0.1875 to 0.1875
- caption_vectors: bfloat16 [1024, 1024], P('dp'), may hold values from -6 to 6
- loss_params: float32 [2], replicated, may hold values from -1 to 1
Outputs:
- image_embedding: float32 [256, 1024], P('dp')
- pair_loss: float32 [256], P('dp')
Inputs may be any that keep to these rules, and one draw needn't show every extreme that they name: `selection`: exactly 128 examples are selected in all; each index of dp holds between 1 and 3 of them, and some holds exactly 3. Among selected examples, at most 4 have the same destination, some destination has exactly 4, and no index of dp holds two selected examples with the same destination. Destinations of unselected examples are arbitrary.
All inputs are finite; a program needn't handle non-finite values.
Results may differ from a plain program's by a relative error of at most 0.0031.
Values may be sent and summed in bfloat16 or wider, within the bound.
A program may use at most 128 MiB of HBM per device.

v0:
```python
import jax
import jax.numpy as jnp
from jax import lax
from jax.sharding import PartitionSpec as P

HEAD_DIM = 64
PATCHES = 256
SEL_DEV = 2
SEND_MOST = 3
RECV_MOST = 4


EPS = 1e-06


def laid_out(blocks, dim):
    blocks = jnp.moveaxis(blocks, 0, dim)
    shape = blocks.shape
    return blocks.reshape(*shape[:dim], shape[dim] * shape[dim + 1], *shape[dim + 2 :])


def copy_for_each(x, axis):
    copies = jnp.broadcast_to(x, (lax.axis_size(axis), *x.shape))
    return lax.all_to_all(copies, axis, split_axis=0, concat_axis=0, tiled=True)


def collect(x, axis, dim):
    return laid_out(copy_for_each(x, axis), dim)


def in_blocks(x, dim, length):
    before, after = (x.shape[:dim], x.shape[dim + 1 :])
    return jnp.moveaxis(x.reshape(*before, length, -1, *after), dim, 0)


def sum_at_owner(x, axis, dim):
    length = lax.axis_size(axis)
    blocks = lax.all_to_all(in_blocks(x, dim, length), axis, 0, 0, tiled=True)
    return jnp.sum(blocks, axis=0)


def of_everyone(x, axis):
    return copy_for_each(x, axis).sum(axis=0)


def layer_norm(values, gain):
    center = jnp.mean(values, axis=-1, keepdims=True)
    centred = values - center
    spread = jnp.mean(centred * centred, axis=-1, keepdims=True)
    return centred * lax.rsqrt(spread + EPS) * gain


def unit_rows(values):
    scale = lax.rsqrt(jnp.mean(values * values, axis=-1, keepdims=True) + EPS)
    return values * scale * values.shape[-1] ** (-0.5)


def compact(members, labels, capacity):
    present = (labels > 0).astype(jnp.int32)
    running = jnp.cumsum(present)
    wanted = jnp.arange(capacity, dtype=jnp.int32)
    source = jnp.sum((running[None, :] <= wanted[:, None]).astype(jnp.int32), axis=1)
    source = jnp.minimum(source, labels.shape[0] - 1)
    filled = wanted < running[-1]
    picked = tuple((member[source] for member in members))
    return (picked, jnp.where(filled, labels[source] - 1, -1).astype(jnp.int32))


def encode(
    images,
    patch_weight,
    position,
    query_key_value,
    output_weight,
    up_weight,
    down_weight,
    norm_gains,
):
    hidden = jnp.einsum("rpc,cd->prd", images, patch_weight, preferred_element_type=jnp.float32)
    hidden = hidden + position.astype(jnp.float32)[:, None, :]
    normed = layer_norm(hidden, norm_gains[0]).astype(jnp.bfloat16)
    projected = jnp.einsum(
        "prd,tdk->rptk",
        collect(normed, "mp", 0),
        query_key_value,
        preferred_element_type=jnp.float32,
    ).astype(jnp.bfloat16)
    image_count = projected.shape[0]
    length = projected.shape[1]
    heads_here = projected.shape[3] // HEAD_DIM
    shaped = projected.reshape(image_count, length, 3, heads_here, HEAD_DIM)
    scores = jnp.einsum(
        "rqhd,rkhd->rhqk", shaped[:, :, 0], shaped[:, :, 1], preferred_element_type=jnp.float32
    ) * HEAD_DIM ** (-0.5)
    weights = jax.nn.softmax(scores, axis=-1).astype(jnp.bfloat16)
    context = jnp.einsum(
        "rhqk,rkhd->rqhd", weights, shaped[:, :, 2], preferred_element_type=jnp.float32
    ).astype(jnp.bfloat16)
    context = context.reshape(image_count, length, heads_here * HEAD_DIM)
    segment = context
    hidden = hidden + sum_at_owner(
        jnp.einsum("rpk,kd->prd", segment, output_weight, preferred_element_type=jnp.float32),
        "mp",
        0,
    )
    normed = layer_norm(hidden, norm_gains[1]).astype(jnp.bfloat16)
    expanded = jax.nn.gelu(
        jnp.einsum(
            "prd,df->prf", collect(normed, "mp", 0), up_weight, preferred_element_type=jnp.float32
        )
    ).astype(jnp.bfloat16)
    segment = expanded
    hidden = hidden + lax.psum_scatter(
        jnp.einsum("prf,fd->prd", segment, down_weight, preferred_element_type=jnp.float32),
        "mp",
        scatter_dimension=0,
        tiled=True,
    )
    return of_everyone(jnp.sum(hidden, axis=0), "mp") / PATCHES


def per_device(
    pixels,
    selection,
    destination,
    patch_weight,
    position,
    query_key_value,
    output_weight,
    up_weight,
    down_weight,
    norm_gains,
    embedding_weight,
    caption_vectors,
    loss_params,
):
    devices_dp = lax.axis_size("dp")
    local_count = selection.shape[0]
    example_ids = lax.axis_index("dp") * local_count + jnp.arange(local_count, dtype=jnp.int32)
    chosen = selection > 0
    local_rank = jnp.cumsum(selection) - 1
    layer_weights = (
        patch_weight,
        position,
        query_key_value,
        output_weight,
        up_weight,
        down_weight,
        norm_gains,
    )
    picker = chosen[None, :] & (
        local_rank[None, :] == jnp.arange(SEND_MOST, dtype=jnp.int32)[:, None]
    )
    caption_rows = jnp.dot(
        picker.astype(jnp.bfloat16), caption_vectors, preferred_element_type=jnp.float32
    ).astype(jnp.bfloat16)
    caption_ids = jnp.sum(jnp.where(picker, example_ids[None, :] + 1, 0), axis=1) - 1
    all_captions, all_caption_ids = (collect(caption_rows, "dp", 0), collect(caption_ids, "dp", 0))
    sorter = (destination[None, :] == jnp.arange(devices_dp, dtype=jnp.int32)[:, None]) & chosen[
        None, :
    ]
    outgoing = jnp.einsum(
        "se,epc->spc", sorter.astype(jnp.bfloat16), pixels, preferred_element_type=jnp.float32
    ).astype(jnp.bfloat16)
    tagged_ids = jnp.sum(jnp.where(sorter, example_ids[None, :] + 1, 0), axis=1)
    arrived, arrived_ids = (
        lax.all_to_all(outgoing, "dp", split_axis=0, concat_axis=0, tiled=True),
        lax.all_to_all(tagged_ids, "dp", split_axis=0, concat_axis=0, tiled=True),
    )
    picked, slot_ids = compact((arrived,), arrived_ids, RECV_MOST)
    pooled = encode(picked[0], *layer_weights)
    live = slot_ids >= 0
    normed = layer_norm(pooled, norm_gains[2]).astype(jnp.bfloat16)
    embedded = jnp.dot(normed, embedding_weight, preferred_element_type=jnp.float32)
    embedded = jnp.where(live[:, None], embedded, 0.0)
    images_unit = unit_rows(embedded)
    captions_unit = unit_rows(all_captions.astype(jnp.float32))
    scale = 10.0 * jnp.exp(loss_params[0])
    shift = 2.0 * loss_params[1]
    logits = scale * jnp.dot(images_unit, captions_unit.T, precision=lax.Precision.HIGHEST) + shift
    signs = jnp.where(slot_ids[:, None] == all_caption_ids[None, :], 1.0, -1.0).astype(jnp.float32)
    caption_live = (all_caption_ids >= 0).astype(jnp.float32)
    terms = jax.nn.softplus(-signs * logits) * caption_live[None, :]
    losses = jnp.where(live, jnp.sum(terms, axis=1) / float(devices_dp * SEL_DEV), 0.0)
    return (embedded, losses)


def solution(mesh):
    in_specs = (
        P("dp", "mp", None),
        P("dp"),
        P("dp"),
        P(),
        P("mp", None),
        P(None, None, "mp"),
        P("mp", None),
        P(None, "mp"),
        P("mp", None),
        P(),
        P(),
        P("dp", None),
        P(),
    )
    out_specs = (P("dp", None), P("dp"))
    return jax.shard_map(
        per_device, mesh=mesh, in_specs=in_specs, out_specs=out_specs, check_vma=False
    )
```

profile of v0, /device:TPU:1, one launch (start us, length us, event | category | flops | bytes accessed | tf_op | source)
XLA Modules:
  0.0 391.6 jit_solution(17666597742640930990)
XLA Ops:
  9.4 13.1 %all-to-all-start = ((s32[64,1,1]{2,1,0:T(1,128)}), s32[64,1,1]{2,1,0:T(1,128)S(1)}, u32[]{:S(2)}, u32[]{:S(2)}) async-start(s32[64,1,1]{2,1,0:T(1,128)} %copy.73), calls=%async_computation | async-start | bytes 65536 | tf_op jit(solution)/shard_map/all_to_all | solution.py:168
  22.6 3.3 convolution_convert_fusion
  25.9 6.2 %copy.76 = bf16[64,64,768]{2,1,0:T(8,128)(2,1)} copy(bf16[64,64,768]{2,0,1:T(8,128)(2,1)S(1)} %convolution_convert_fusion) | data formatting | bytes 12582912 | tf_op jit(solution)/shard_map/convert_element_type | solution.py:164
  32.2 10.6 %all-to-all-start.1 = ((bf16[64,64,768]{2,1,0:T(8,128)(2,1)}), bf16[64,64,768]{2,1,0:T(8,128)(2,1)}, u32[]{:S(2)}, u32[]{:S(2)}) async-start(bf16[64,64,768]{2,1,0:T(8,128)(2,1)} %copy.76), calls=%async_computation.1 | async-start | bytes 12582912 | tf_op jit(solution)/shard_map/all_to_all | solution.py:167
  43.3 138.4 %all-to-all-done.1 = bf16[64,64,768]{2,1,0:T(8,128)(2,1)} async-done(((bf16[64,64,768]{2,1,0:T(8,128)(2,1)}), bf16[64,64,768]{2,1,0:T(8,128)(2,1)}, u32[]{:S(2)}, u32[]{:S(2)}) %all-to-all-start.1) | async-done | bytes 6291488 | tf_op jit(solution)/shard_map/all_to_all | solution.py:167
  181.6 3.4 gather_fusion.1
  185.0 2.1 fusion.81
  188.5 27.0 %all_to_all.48 = bf16[4,64,4,1024]{3,1,2,0:T(8,128)(2,1)S(1)} all-to-all(bf16[4,64,4,1024]{3,1,2,0:T(8,128)(2,1)S(1)} %broadcast_in_dim.94), channel_id=1, replica_groups=mesh['dp'=64,'mp'=4] {'mp'}, dimensions={0} | all-to-all | bytes 4194304 | tf_op jit(solution)/shard_map/all_to_all | solution.py:24
  217.0 1.9 convolution_convert_fusion.1
  219.6 3.2 fusion.82
  225.2 48.2 %all_to_all.49 = f32[4,64,4,1024]{3,1,2,0:T(8,128)} all-to-all(f32[4,64,4,1024]{3,1,2,0:T(8,128)S(1)} %copy.84), channel_id=1, replica_groups=mesh['dp'=64,'mp'=4] {'mp'}, dimensions={0} | all-to-all | bytes 8388608 | tf_op jit(solution)/shard_map/all_to_all | solution.py:38
  273.4 3.7 reduce_sum.149
  277.2 1.7 fusion.78
  279.7 23.7 %all_to_all.50 = bf16[4,64,4,1024]{3,1,2,0:T(8,128)(2,1)S(1)} all-to-all(bf16[4,64,4,1024]{3,1,2,0:T(8,128)(2,1)S(1)} %broadcast_in_dim.95), channel_id=1, replica_groups=mesh['dp'=64,'mp'=4] {'mp'}, dimensions={0} | all-to-all | bytes 4194304 | tf_op jit(solution)/shard_map/all_to_all | solution.py:24
  303.3 1.5 copy.85
  304.8 8.7 %fusion.12 = f32[256,4,1024]{2,0,1:T(8,128)} fusion(bf16[1024,1024]{1,0:T(8,128)(2,1)S(1)} %copy-done, bf16[256,4,1024]{2,0,1:T(8,128)(2,1)} %bitcast.81, bf16[1024,1024]{1,0:T(8,128)(2,1)} %param.20), kind=kOutput, calls=%fused_computation.17 | convolution fusion | flops 4304404480 | bytes 10485760 | tf_op jit(solution)/shard_map/prf,fd->prd/dot_general | solution.py:114
  315.2 19.1 %all-to-all-start.6 = ((s32[64,1,3]{2,1,0:T(1,128)}), s32[64,1,3]{2,1,0:T(1,128)S(1)}, u32[]{:S(2)}, u32[]{:S(2)}) async-start(s32[64,1,3]{2,1,0:T(1,128)} %broadcast_in_dim.100), calls=%async_computation.7 | async-start | bytes 65536 | tf_op jit(solution)/shard_map/all_to_all | solution.py:24
  334.5 9.3 %all-to-all-done.6 = s32[64,1,3]{2,1,0:T(1,128)S(1)} async-done(((s32[64,1,3]{2,1,0:T(1,128)}), s32[64,1,3]{2,1,0:T(1,128)S(1)}, u32[]{:S(2)}, u32[]{:S(2)}) %all-to-all-start.6) | async-done | bytes 800 | tf_op jit(solution)/shard_map/all_to_all | solution.py:24
  344.7 5.5 %all-to-all-start.7 = ((bf16[64,3,1024]{2,1,0:T(4,128)(2,1)}), bf16[64,3,1024]{2,1,0:T(4,128)(2,1)}, u32[]{:S(2)}, u32[]{:S(2)}) async-start(bf16[64,3,1024]{2,1,0:T(4,128)(2,1)} %broadcast_in_dim.103), calls=%async_computation.8 | async-start | bytes 1048576 | tf_op jit(solution)/shard_map/all_to_all | solution.py:24
  356.6 11.3 %all-to-all-done.7 = bf16[64,3,1024]{2,1,0:T(4,128)(2,1)} async-done(((bf16[64,3,1024]{2,1,0:T(4,128)(2,1)}), bf16[64,3,1024]{2,1,0:T(4,128)(2,1)}, u32[]{:S(2)}, u32[]{:S(2)}) %all-to-all-start.7) | async-done | bytes 393248 | tf_op jit(solution)/shard_map/all_to_all | solution.py:24
  369.4 1.6 reduce-scatter.2.cloned.1.call-done
  373.0 3.3 all-to-all-start.5
  377.8 2.9 all-to-all-done.5
  381.1 2.1 multiply_reduce_fusion.4
  (81 shorter events, 23.8 us)
Async XLA Ops:
  7.2 297.7 %copy-start = (bf16[1024,1024]{1,0:T(8,128)(2,1)S(1)}, bf16[1024,1024]{1,0:T(8,128)(2,1)}, u32[]{:S(2)}) copy-start(bf16[1024,1024]{1,0:T(8,128)(2,1)} %param.21) | copy-start | bytes 6291460
  9.4 22.7 %all-to-all-start = ((s32[64,1,1]{2,1,0:T(1,128)}), s32[64,1,1]{2,1,0:T(1,128)S(1)}, u32[]{:S(2)}, u32[]{:S(2)}) async-start(s32[64,1,1]{2,1,0:T(1,128)} %copy.73), calls=%async_computation | async-start | bytes 65536 | tf_op jit(solution)/shard_map/all_to_all | solution.py:168
  32.2 10.7 %copy-start.3 = (bf16[64,1024]{1,0:T(8,128)(2,1)S(1)}, bf16[64,1024]{1,0:T(8,128)(2,1)}, u32[]{:S(2)}) copy-start(bf16[64,1024]{1,0:T(8,128)(2,1)} %param.17) | copy-start | bytes 393220
  32.2 10.7 %copy-start.6 = (f32[3,1024]{1,0:T(4,128)S(1)}, f32[3,1024]{1,0:T(4,128)}, u32[]{:S(2)}) copy-start(f32[3,1024]{1,0:T(4,128)} %param.22) | copy-start | bytes 36868
  32.2 149.5 %all-to-all-start.1 = ((bf16[64,64,768]{2,1,0:T(8,128)(2,1)}), bf16[64,64,768]{2,1,0:T(8,128)(2,1)}, u32[]{:S(2)}, u32[]{:S(2)}) async-start(bf16[64,64,768]{2,1,0:T(8,128)(2,1)} %copy.76), calls=%async_computation.1 | async-start | bytes 12582912 | tf_op jit(solution)/shard_map/all_to_all | solution.py:167
  42.8 328.2 %reduce-scatter.2.cloned.1.call-start = ((), (), s32[]{:S(2)}) async-start(), calls=%async_computation.9 | async-start | bytes 5242880 | tf_op jit(solution)/shard_map/reduce_scatter | solution.py:113
  187.1 1.0 copy-start.1
  215.5 1.4 copy-start.9
  222.8 1.0 copy-start.2
  313.6 0.7 copy-start.8
  313.6 20.8 %copy-start.5 = (bf16[16,1024]{1,0:T(8,128)(2,1)S(1)}, bf16[16,1024]{1,0:T(8,128)(2,1)}, u32[]{:S(2)}) copy-start(bf16[16,1024]{1,0:T(8,128)(2,1)} %param.24) | copy-start | bytes 98308
  313.6 36.7 %copy-start.7 = (f32[2]{0:T(128)S(1)}, f32[2]{0:T(128)}, u32[]{:S(2)}) copy-start(f32[2]{0:T(128)} %param.25) | copy-start | bytes 28
  315.2 28.6 %all-to-all-start.6 = ((s32[64,1,3]{2,1,0:T(1,128)}), s32[64,1,3]{2,1,0:T(1,128)S(1)}, u32[]{:S(2)}, u32[]{:S(2)}) async-start(s32[64,1,3]{2,1,0:T(1,128)} %broadcast_in_dim.100), calls=%async_computation.7 | async-start | bytes 65536 | tf_op jit(solution)/shard_map/all_to_all | solution.py:24
  344.7 23.2 %all-to-all-start.7 = ((bf16[64,3,1024]{2,1,0:T(4,128)(2,1)}), bf16[64,3,1024]{2,1,0:T(4,128)(2,1)}, u32[]{:S(2)}, u32[]{:S(2)}) async-start(bf16[64,3,1024]{2,1,0:T(4,128)(2,1)} %broadcast_in_dim.103), calls=%async_computation.8 | async-start | bytes 1048576 | tf_op jit(solution)/shard_map/all_to_all | solution.py:24
  373.0 7.7 %all-to-all-start.5 = ((f32[4,4,1024]{2,1,0:T(4,128)}), f32[4,4,1024]{2,1,0:T(4,128)S(1)}, u32[]{:S(2)}, u32[]{:S(2)}) async-start(f32[4,4,1024]{2,1,0:T(4,128)} %broadcast_in_dim.96), calls=%async_computation.6 | async-start | bytes 131072 | tf_op jit(solution)/shard_map/all_to_all | solution.py:24
  383.3 1.5 copy-start.4
Sparse Core Ops, SparseCore 0:
  313.7 57.2 reduce-scatter.1
where the time goes:
time: 393 us; the launch traced here: 392 us
  waiting for transfers between devices  164 us (42%)
  blocking collectives  98.9 us (25%)
  starting transfers between devices  51.7 us (13%)
  local copies, waits for them, and re-layouts  22.3 us (6%)
  matrix products  21.2 us (5%)
  other arithmetic  18.2 us (5%)
  between operations  15.7 us (4%)
    all_to_all x1, waiting for transfers between devices, per_device(): lax.all_to_all(outgoing, 'dp', split_axis=0, concat_axis=0, tiled=True)  138 us
    all_to_all x2, blocking collectives, copy_for_each(): return lax.all_to_all(copies, axis, split_axis=0, concat_axis=0, tiled=True)  50.7 us
    all_to_all x1, blocking collectives, sum_at_owner(): blocks = lax.all_to_all(in_blocks(x, dim, length), axis, 0, 0, tiled=True)  48.2 us
    all_to_all x3, starting transfers between devices, copy_for_each(): return lax.all_to_all(copies, axis, split_axis=0, concat_axis=0, tiled=True)  28 us
    all_to_all x3, waiting for transfers between devices, copy_for_each(): return lax.all_to_all(copies, axis, split_axis=0, concat_axis=0, tiled=True)  23.5 us
    all_to_all x1, starting transfers between devices, per_device(): lax.all_to_all(tagged_ids, 'dp', split_axis=0, concat_axis=0, tiled=True)  13.1 us
    all_to_all x1, starting transfers between devices, per_device(): lax.all_to_all(outgoing, 'dp', split_axis=0, concat_axis=0, tiled=True)  10.6 us
    dot_general x1, matrix products, encode(): jnp.einsum('prf,fd->prd', segment, down_weight, preferred_element_type=jn...  8.72 us
  transfers between devices with their start and end apart: 6, of which 5 were waited for; matrix products, arithmetic and copies ran while one was open for 5% of the time, Pallas kernels for 0%

commit v1 on v0

v1 whole, which is shorter than its diff:
```python
import jax
import jax.numpy as jnp
from jax import lax
from jax.sharding import PartitionSpec as P

HEAD_DIM = 64
PATCHES = 256
SEL_DEV = 2
SEND_MOST = 3
RECV_MOST = 4
EPS = 1e-06


def layer_norm(values, gain):
    center = jnp.mean(values, axis=-1, keepdims=True)
    centred = values - center
    spread = jnp.mean(centred * centred, axis=-1, keepdims=True)
    return centred * lax.rsqrt(spread + EPS) * gain


def unit_rows(values):
    scale = lax.rsqrt(jnp.mean(values * values, axis=-1, keepdims=True) + EPS)
    return values * scale * values.shape[-1] ** (-0.5)


def per_device(
    pixels, selection, destination, patch_weight, position, query_key_value, output_weight,
    up_weight, down_weight, norm_gains, embedding_weight, caption_vectors, loss_params,
):
    n_dp = lax.axis_size("dp")
    f32, bf16 = jnp.float32, jnp.bfloat16
    chosen = selection > 0
    local_rank = jnp.cumsum(selection) - 1
    picker = chosen[None, :] & (local_rank[None, :] == jnp.arange(SEND_MOST, dtype=jnp.int32)[:, None])
    live = jnp.any(picker, axis=1)
    dest = jnp.sum(jnp.where(picker, destination[None, :] + 1, 0), axis=1) - 1
    index = jnp.sum(jnp.where(picker, jnp.arange(selection.shape[0], dtype=jnp.int32)[None, :], 0), axis=1)

    captions = jnp.dot(picker.astype(bf16), caption_vectors, preferred_element_type=f32).astype(bf16)
    all_captions = lax.all_gather(captions, "dp", axis=0, tiled=True)
    all_dest = lax.all_gather(dest, "dp", axis=0, tiled=True)

    image = jnp.stack([lax.dynamic_index_in_dim(pixels, index[k], 0, keepdims=False) for k in range(SEND_MOST)])
    image = lax.all_gather(image, "mp", axis=1, tiled=True)
    place = lax.all_gather(position, "mp", axis=0, tiled=True)
    output_all = lax.all_gather(output_weight, "mp", axis=0, tiled=True)

    hidden = jnp.einsum("rpc,cd->rpd", image, patch_weight, preferred_element_type=f32) + place.astype(f32)[None]
    normed = layer_norm(hidden, norm_gains[0]).astype(bf16)
    projected = jnp.einsum("rpd,tdk->trpk", normed, query_key_value, preferred_element_type=f32).astype(bf16)
    heads = projected.shape[-1] // HEAD_DIM
    shaped = projected.reshape(3, SEND_MOST, PATCHES, heads, HEAD_DIM)
    scores = jnp.einsum("rqhd,rkhd->rhqk", shaped[0], shaped[1], preferred_element_type=f32) * HEAD_DIM ** (-0.5)
    weights = jax.nn.softmax(scores, axis=-1).astype(bf16)
    context = jnp.einsum("rhqk,rkhd->rqhd", weights, shaped[2], preferred_element_type=f32).astype(bf16)
    context = context.reshape(SEND_MOST, PATCHES, heads * HEAD_DIM)
    context = lax.all_gather(context, "mp", axis=0)
    segments = output_all.reshape(lax.axis_size("mp"), -1, output_all.shape[-1])
    hidden = hidden + jnp.einsum("mrpk,mkd->rpd", context, segments, preferred_element_type=f32)
    normed = layer_norm(hidden, norm_gains[1]).astype(bf16)
    expanded = jax.nn.gelu(jnp.einsum("rpd,df->rpf", normed, up_weight, preferred_element_type=f32)).astype(bf16)
    summed = jnp.sum(expanded.astype(f32), axis=1)
    part = jnp.dot(summed, down_weight.astype(f32), precision=lax.Precision.HIGHEST)
    rows = PATCHES // lax.axis_size("mp")
    own = lax.dynamic_slice_in_dim(hidden, lax.axis_index("mp") * rows, rows, axis=1)
    part = part + jnp.sum(own, axis=1)
    pooled = jnp.sum(lax.all_gather(part, "mp", axis=0), axis=0) / PATCHES
    normed = layer_norm(pooled, norm_gains[2]).astype(bf16)

    sorter = (dest[None, :] == jnp.arange(n_dp, dtype=jnp.int32)[:, None]) & live[None, :]
    outgoing = jnp.dot(sorter.astype(bf16), normed, preferred_element_type=f32).astype(bf16)
    arrived = lax.all_to_all(outgoing, "dp", split_axis=0, concat_axis=0, tiled=True)

    match = (all_dest == lax.axis_index("dp")).astype(jnp.int32).reshape(n_dp, SEND_MOST)
    present = jnp.sum(match, axis=1)
    place_of = jnp.cumsum(present) - present
    pick = (present[None, :] > 0) & (place_of[None, :] == jnp.arange(RECV_MOST, dtype=jnp.int32)[:, None])
    filled = jnp.any(pick, axis=1)
    slots = jnp.dot(pick.astype(bf16), arrived, preferred_element_type=f32).astype(bf16)
    embedded = jnp.dot(slots, embedding_weight, preferred_element_type=f32)
    embedded = jnp.where(filled[:, None], embedded, 0.0)
    scale = 10.0 * jnp.exp(loss_params[0])
    shift = 2.0 * loss_params[1]
    logits = scale * jnp.dot(
        unit_rows(embedded), unit_rows(all_captions.astype(f32)).T, precision=lax.Precision.HIGHEST
    ) + shift
    same = (pick[:, :, None] & (match[None] > 0)).reshape(RECV_MOST, n_dp * SEND_MOST)
    signs = jnp.where(same, 1.0, -1.0)
    terms = jax.nn.softplus(-signs * logits) * (all_dest >= 0).astype(f32)[None, :]
    losses = jnp.where(filled, jnp.sum(terms, axis=1) / float(n_dp * SEL_DEV), 0.0)
    return embedded, losses


def solution(mesh):
    in_specs = (
        P("dp", "mp", None), P("dp"), P("dp"), P(), P("mp", None), P(None, None, "mp"), P("mp", None),
        P(None, "mp"), P("mp", None), P(), P(), P("dp", None), P(),
    )
    out_specs = (P("dp", None), P("dp"))
    return jax.shard_map(per_device, mesh=mesh, in_specs=in_specs, out_specs=out_specs, check_vma=False)
```

time: 393 us -> 189 us (0.48)
  waiting for transfers between devices: 164 us -> 24.9 us
  starting transfers between devices: 51.7 us -> 10.2 us
  local copies, waits for them, and re-layouts: 22.3 us -> 9.66 us
  other arithmetic: 18.2 us -> 6.19 us
  between operations: 15.7 us -> 22 us
  blocking collectives: 98.9 us -> 93.9 us
    all_to_all x1, waiting for transfers between devices: 138 us -> 8.89 us  [per_device(): lax.all_to_all(outgoing, 'dp', split_axis=0, concat_axis=0, tiled=True)]
    all_to_all x3 -> x0, blocking collectives: 98.9 us -> none  [the longest x2 50.7 us: copy_for_each(): return lax.all_to_all(copies, axis, split_axis=0, concat_axis=0, tiled=True)]
    all_gather x0 -> x3, blocking collectives: none -> 73.5 us  [the longest x1 52.1 us: per_device(): all_captions = lax.all_gather(captions, 'dp', axis=0, tiled=True)]
    all_to_all x4 -> x0, starting transfers between devices: 41.1 us -> none  [the longest x3 28 us: copy_for_each(): return lax.all_to_all(copies, axis, split_axis=0, concat_axis=0, tiled=True)]
    all_to_all x4 -> x0, waiting for transfers between devices: 23.5 us -> none  [the longest x3 23.5 us: copy_for_each(): return lax.all_to_all(copies, axis, split_axis=0, concat_axis=0, tiled=True)]
    unnamed x0 -> x1, blocking collectives: none -> 20.4 us
    all_gather x0 -> x3, waiting for transfers between devices: none -> 15.3 us  [the longest x1 15.3 us: per_device(): image = lax.all_gather(image, 'mp', axis=1, tiled=True)]
    convert_element_type x2 -> x1, local copies, waits for them, and re-layouts: 7.57 us -> 0.29 us  [per_device(): all_captions.astype(f32)]
  transfers between devices with their start and end apart: 6 -> 4, of which waited for: 5 -> 2; matrix products, arithmetic and copies ran while one was open for 5% -> 8% of each run, Pallas kernels for 0% -> 0%
where the time goes in v1:
time: 189 us; the launch traced here: 188 us
  blocking collectives  93.9 us (50%)
  waiting for transfers between devices  24.9 us (13%)
  between operations  22 us (12%)
  matrix products  21.3 us (11%)
  starting transfers between devices  10.2 us (5%)
  local copies, waits for them, and re-layouts  9.66 us (5%)
  other arithmetic  6.19 us (3%)
    all_gather x1, blocking collectives, per_device(): all_captions = lax.all_gather(captions, 'dp', axis=0, tiled=True)  52.1 us
    unnamed x1, blocking collectives  20.4 us
    all_gather x1, waiting for transfers between devices, per_device(): image = lax.all_gather(image, 'mp', axis=1, tiled=True)  15.3 us
    all_gather x1, blocking collectives, per_device(): place = lax.all_gather(position, 'mp', axis=0, tiled=True)  12.5 us
    all_to_all x1, starting transfers between devices, per_device(): lax.all_to_all(outgoing, 'dp', split_axis=0, concat_axis=0, tiled=True)  10 us
    all_gather x1, blocking collectives, per_device(): pooled = jnp.sum(lax.all_gather(part, 'mp', axis=0), axis=0) / PATCHES  8.97 us
    all_to_all x1, waiting for transfers between devices, per_device(): lax.all_to_all(outgoing, 'dp', split_axis=0, concat_axis=0, tiled=True)  8.89 us
    dot_general x1, matrix products, per_device(): jnp.einsum('mrpk,mkd->rpd', context, segments, preferred_element_type=f32)  5.1 us
  transfers between devices with their start and end apart: 4, of which 2 were waited for; matrix products, arithmetic and copies ran while one was open for 8% of the time, Pallas kernels for 0%

profile of v1, /device:TPU:1, one launch (start us, length us, event | category | flops | bytes accessed | tf_op | source)
XLA Modules:
  0.0 188.1 jit_solution(4609021758718230492)
XLA Ops:
  7.2 0.8 broadcast_compare_fusion.2
  8.0 0.7 copy.37
  16.5 1.0 constant_dynamic-slice_fusion.2
  17.5 0.8 pad_maximum_fusion
  18.3 0.7 all-gather.11.cloned.1.call-update
  19.1 12.5 %all_gather.26 = bf16[256,1024]{1,0:T(8,128)(2,1)S(1)} all-gather(bf16[64,1024]{1,0:T(8,128)(2,1)} %param.17), channel_id=1, replica_groups=mesh['dp'=64,'mp'=4] {'mp'}, dimensions={0}, use_global_device_ids=true | all-gather | bytes 655360 | tf_op jit(solution)/shard_map/all_gather | solution.py:45
  31.7 15.3 %all-gather.7.cloned.1.call-done = bf16[3,256,768]{2,1,0:T(8,128)(2,1)} async-done(((bf16[3,64,768]{2,1,0:T(8,128)(2,1)}), bf16[3,256,768]{2,1,0:T(8,128)(2,1)}) %all-gather.7.cloned.1.call-update) | async-done | bytes 1179664 | tf_op jit(solution)/shard_map/all_gather | solution.py:44
  47.0 3.3 %add_reduce_fusion = (f32[3,256]{1,0:T(4,128)S(1)}, f32[3,256,1024]{2,1,0:T(8,128)S(1)}) fusion(f32[256,1024]{1,0:T(8,128)S(1)} %convert_element_type.56, bf16[3,256,768]{2,1,0:T(8,128)(2,1)} %all-gather.7.cloned.1.call-done, bf16[768,1024]{1,0:T(8,128)(2,1)} %param.16), kind=kOutput, calls=%fused_computation.20 | convolution fusion | flops 1209531648 | bytes 6949888 | tf_op jit(solution)/shard_map/rpc,cd->rpd/dot_general | solution.py:48
  51.0 1.9 copy-done.9
  52.8 2.1 %fusion.36 = bf16[3,3,256,256]{2,3,0,1:T(8,128)(2,1)S(1)} fusion(bf16[3,1024,256]{2,1,0:T(8,128)(2,1)S(1)} %copy-done.9, f32[3,256,1024]{2,1,0:T(8,128)S(1)} %get-tuple-element.28, f32[1024]{0:T(1024)S(1)} %bitcast.85, f32[3,256]{1,0:T(4,128)S(1)} %add_rsqrt_fusion.1, f32[3,256]{1,0:T(4,128)S(1)} %broadcast_multiply_fusion.1, ...), kind=kOutput, calls=%fused_computation.38 | convolution fusion | flops 1212481536 | bytes 6957056 | tf_op jit(solution)/shard_map/rpd,tdk->trpk/dot_general | solution.py:50
  55.0 2.9 %fusion.91 = (f32[3,4,256]{2,1,0:T(4,128)S(1)}, f32[3,4,256,256]{2,3,1,0:T(8,128)}) fusion(bf16[3,256,4,64]{1,3,2,0:T(8,128)(2,1)S(1)} %bitcast.81, bf16[3,256,4,64]{1,3,2,0:T(8,128)(2,1)S(1)} %bitcast.80), kind=kOutput, calls=%fused_computation.116 | convolution fusion | flops 103022848 | bytes 3944448 | tf_op jit(solution)/shard_map/sub | solution.py:54
  57.9 2.3 %fusion.41 = bf16[3,4,64,256]{3,2,1,0:T(8,128)(2,1)S(1)} fusion(bf16[3,256,4,64]{1,3,2,0:T(8,128)(2,1)S(1)} %bitcast.79, f32[3,4,256,256]{2,3,1,0:T(8,128)} %get-tuple-element.30, f32[3,4,256]{2,1,0:T(4,128)S(1)} %get-tuple-element.29), kind=kOutput, calls=%fused_computation.39 | convolution fusion | flops 102432768 | bytes 3944448 | tf_op jit(solution)/shard_map/rhqk,rkhd->rqhd/dot_general | solution.py:55
  60.2 0.9 copy.41
  62.5 20.4 %all-reduce = s32[192]{0:T(256)S(1)} all-reduce(s32[192]{0:T(256)S(1)} %get-tuple-element.26), channel_id=1, replica_groups=mesh['dp'=64,'mp'=4] {'dp'}, use_global_device_ids=true, to_apply=%add | all-reduce | flops 192 | bytes 1536
  83.6 52.1 %all-gather.2 = bf16[64,3,1024]{2,1,0:T(4,128)(2,1)S(1)} all-gather(bf16[1,3,1024]{2,1,0:T(4,128)(2,1)S(1)} %fusion.44), channel_id=1, replica_groups=mesh['dp'=64,'mp'=4] {'dp'}, dimensions={0}, use_global_device_ids=true | all-gather | bytes 399360 | tf_op jit(solution)/shard_map/all_gather | solution.py:40
  136.3 5.1 %fusion.92 = (f32[3,256]{1,0:T(4,128)S(1)}, f32[3,256,1024]{2,1,0:T(8,128)S(1)}) fusion(bf16[4,3,256,256]{3,2,0,1:T(8,128)(2,1)} %all-gather.9.cloned.1.call-done, bf16[4,256,1024,1]{2,1,0,3:T(8,128)(2,1)} %bitcast.88, f32[3,256,1024]{2,1,0:T(8,128)} %copy-done.2, f32[256,1024]{1,0:T(8,128)} %copy-done.1), kind=kOutput, calls=%fused_computation.117 | convolution fusion | flops 1612971264 | bytes 11013120 | tf_op jit(solution)/shard_map/mrpk,mkd->rpd/dot_general | solution.py:59
  142.0 1.0 copy-done.8
  143.0 2.8 %convert_reduce_fusion = f32[3,1024]{1,0:T(4,128)S(1)} fusion(bf16[1024,1024]{1,0:T(8,128)(2,1)S(1)} %copy-done.8, f32[3,256,1024]{2,1,0:T(8,128)S(1)} %get-tuple-element.32, f32[1024]{0:T(1024)S(1)} %bitcast.84, f32[3,256]{1,0:T(4,128)S(1)} %add_rsqrt_fusion, f32[3,256]{1,0:T(4,128)S(1)} %broadcast_multiply_fusion), kind=kOutput, calls=%fused_computation.11 | convolution fusion | flops 1622406144 | bytes 5265408 | tf_op jit(solution)/shard_map/rpd,df->rpf/dot_general | solution.py:61
  145.8 0.9 fusion.43
  146.8 9.0 %all-gather.1 = f32[4,3,1024]{2,1,0:T(4,128)S(1)} all-gather(f32[1,3,1024]{2,1,0:T(4,128)S(1)} %fusion.43), channel_id=2, replica_groups=mesh['dp'=64,'mp'=4] {'mp'}, dimensions={0}, use_global_device_ids=true | all-gather | bytes 61440 | tf_op jit(solution)/shard_map/all_gather | solution.py:67
  157.5 0.7 reshape.217
  158.2 10.0 %all-to-all-start = ((bf16[64,2,512]{2,1,0:T(2,128)(2,1)}), bf16[64,2,512]{2,1,0:T(2,128)(2,1)S(1)}, u32[]{:S(2)}, u32[]{:S(2)}) async-start(bf16[64,2,512]{2,1,0:T(2,128)(2,1)} %reshape.217), calls=%async_computation | async-start | bytes 262144 | tf_op jit(solution)/shard_map/all_to_all | solution.py:72
  170.5 8.9 %all-to-all-done = bf16[64,2,512]{2,1,0:T(2,128)(2,1)S(1)} async-done(((bf16[64,2,512]{2,1,0:T(2,128)(2,1)}), bf16[64,2,512]{2,1,0:T(2,128)(2,1)S(1)}, u32[]{:S(2)}, u32[]{:S(2)}) %all-to-all-start) | async-done | bytes 131104 | tf_op jit(solution)/shard_map/all_to_all | solution.py:72
  180.1 0.9 fusion.72
  (74 shorter events, 9.1 us)
Async XLA Ops:
  7.2 172.3 %copy-start = (bf16[1024,1024]{1,0:T(8,128)(2,1)S(1)}, bf16[1024,1024]{1,0:T(8,128)(2,1)}, u32[]{:S(2)}) copy-start(bf16[1024,1024]{1,0:T(8,128)(2,1)} %param.23) | copy-start | bytes 6291460
  7.2 24.5 %copy-start.6 = (f32[3,1024]{1,0:T(4,128)S(1)}, f32[3,1024]{1,0:T(4,128)}, u32[]{:S(2)}) copy-start(f32[3,1024]{1,0:T(4,128)} %param.22) | copy-start | bytes 36868
  7.2 39.8 %all-gather.7.cloned.1.call-start = ((), (), s32[]{:S(2)}) async-start(), calls=%async_computation.1 | async-start | bytes 1474560 | tf_op jit(solution)/shard_map/all_gather | solution.py:44
  18.3 118.0 %all-gather.11.cloned.1.call-start = ((), (), s32[]{:S(2)}) async-start(), calls=%async_computation.3 | async-start | bytes 2621440 | tf_op jit(solution)/shard_map/all_gather | solution.py:46
  19.0 117.3 %all-gather.9.cloned.1.call-start = ((), (), s32[]{:S(2)}) async-start(), calls=%async_computation.2 | async-start | bytes 1966080 | tf_op jit(solution)/shard_map/all_gather | solution.py:57
  31.7 19.3 %copy-start.1 = (f32[256,1024]{1,0:T(8,128)}, f32[256,1024]{1,0:T(8,128)S(1)}, u32[]{:S(2)}) copy-start(f32[256,1024]{1,0:T(8,128)S(1)} %convert_element_type.56) | copy-start | bytes 3145732
  50.3 4.6 %copy-start.2 = (f32[3,256,1024]{2,1,0:T(8,128)}, f32[3,256,1024]{2,1,0:T(8,128)S(1)}, u32[]{:S(2)}) copy-start(f32[3,256,1024]{2,1,0:T(8,128)S(1)} %get-tuple-element.28) | copy-start | bytes 9437188
  50.3 2.5 %copy-start.9 = (bf16[3,1024,256]{2,1,0:T(8,128)(2,1)S(1)}, bf16[3,1024,256]{2,1,0:T(8,128)(2,1)}, u32[]{:S(2)}) copy-start(bf16[3,1024,256]{2,1,0:T(8,128)(2,1)} %param.18) | copy-start | bytes 4718596
  57.9 3.3 %copy-start.10 = (u32[256]{0:T(256)S(1)}, u32[256]{0:T(256)}, u32[]{:S(2)}) copy-start(u32[256]{0:T(256)} %constant.102) | copy-start | bytes 3076
  57.9 25.6 %copy-start.5 = (bf16[16,1024]{1,0:T(8,128)(2,1)S(1)}, bf16[16,1024]{1,0:T(8,128)(2,1)}, u32[]{:S(2)}) copy-start(bf16[16,1024]{1,0:T(8,128)(2,1)} %param.24) | copy-start | bytes 98308
  141.4 1.6 copy-start.8
  143.0 2.8 %copy-start.3 = (bf16[1024,1024]{1,0:T(8,128)(2,1)S(1)}, bf16[1024,1024]{1,0:T(8,128)(2,1)}, u32[]{:S(2)}) copy-start(bf16[1024,1024]{1,0:T(8,128)(2,1)} %param.21) | copy-start | bytes 6291460
  145.8 22.5 %copy-start.7 = (f32[2]{0:T(128)S(1)}, f32[2]{0:T(128)}, u32[]{:S(2)}) copy-start(f32[2]{0:T(128)} %param.25) | copy-start | bytes 28
  158.2 21.1 %all-to-all-start = ((bf16[64,2,512]{2,1,0:T(2,128)(2,1)}), bf16[64,2,512]{2,1,0:T(2,128)(2,1)S(1)}, u32[]{:S(2)}, u32[]{:S(2)}) async-start(bf16[64,2,512]{2,1,0:T(2,128)(2,1)} %reshape.217), calls=%async_computation | async-start | bytes 262144 | tf_op jit(solution)/shard_map/all_to_all | solution.py:72
  180.1 1.5 copy-start.4
Sparse Core Ops, SparseCore 0:
  18.4 28.5 all-gather.6
  48.8 35.8 all-gather.10
  86.5 29.0 all-gather.8

commit v2 on v1

v2 whole, which is shorter than its diff:
```python
import functools

import jax
import jax.numpy as jnp
from jax import lax
from jax.experimental import pallas as pl
from jax.experimental.pallas import tpu as pltpu
from jax.sharding import PartitionSpec as P

EPS = 1e-06
SEND_MOST = 3
RECV_MOST = 4
SEL_DEV = 2
HEAD_DIM = 64
Y, CORES = 4, 2
F32, BF16 = jnp.float32, jnp.bfloat16
NT = (((1,), (1,)), ((), ()))


def norm_rows(values, gain):
    center = jnp.mean(values, axis=-1, keepdims=True)
    centred = values - center
    spread = jnp.mean(centred * centred, axis=-1, keepdims=True)
    return centred * lax.rsqrt(spread + EPS) * gain


def diagonal(rows):
    count = rows.shape[0]
    line = lax.broadcasted_iota(jnp.int32, (count, 128), 0) % 8
    out = jnp.zeros((count, 128), rows.dtype)
    for chunk in range(8):
        out = jnp.where(line == chunk, rows[:, chunk * 128 : (chunk + 1) * 128], out)
    return out


def dot(a, b):
    return jnp.dot(a, b, preferred_element_type=F32)


def body(
    n_dp, n_mp,
    selection, destination, loss_params, pixels, patch_weight, position, query_key_value, output_weight,
    up_weight, down_weight, gains, embedding_weight, captions,
    embedded_out, losses_out,
    pixels_v, patch_v, qkv_v, up_v, down_v, embedding_v, captions_v,
    pix, place, wo, hid, normed, qkv, ctx, cap_send, caps, caps_flat, summed, shared,
    out_send, arrived, picker, sign_of, weight_of,
    local, pix_s, pix_r, px_s, px_r, py_s, py_r, pc_s, pc_r, wx_s, wx_r, wy_s, wy_r, wc_s, wc_r,
    ctx_s, ctx_r, ar_s, ar_r, cap_s, cap_r, out_s, out_r,
):
    dp, mp = lax.axis_index("dp"), lax.axis_index("mp")
    right, left, opposite = (mp + 1) % n_mp, (mp + n_mp - 1) % n_mp, (mp + 2) % n_mp
    core, y, z = dp % CORES, (dp // CORES) % Y, dp // (CORES * Y)

    def on_y(step):
        return (z * Y + (y + step) % Y) * CORES + core

    partner = dp + 1 - 2 * core
    y_up, y_down, y_far = (y + 1) % Y, (y + Y - 1) % Y, (y + 2) % Y

    def remote(src, dst, sends, receives, where):
        return pltpu.make_async_remote_copy(
            src_ref=src, dst_ref=dst, send_sem=sends, recv_sem=receives, device_id=where,
            device_id_type=pl.DeviceIdType.MESH,
        )

    def arrival(ref, receives):
        remote(ref, ref, receives, receives, (dp, right)).wait_recv()

    pending = []

    def send(ref, sends, receives, where, src=None):
        src = ref if src is None else src
        remote(src, ref, sends, receives, where).start()
        pending.append((src, ref, sends, receives, where))

    loads = [
        (pixels, pixels_v), (captions, captions_v), (patch_weight, patch_v), (position, place.at[mp]),
        (query_key_value, qkv_v), (output_weight, wo.at[mp]), (up_weight, up_v), (down_weight, down_v),
        (embedding_weight, embedding_v),
    ]
    loads = [pltpu.make_async_copy(a, b, local.at[n]) for n, (a, b) in enumerate(loads)]
    for load in loads:
        load.start()

    barrier = pltpu.get_barrier_semaphore()

    def greet(step, carry):
        pl.semaphore_signal(barrier, inc=1, device_id=((dp + step) % n_dp, mp), device_id_type=pl.DeviceIdType.MESH)
        return carry

    for other in (right, left, opposite):
        pl.semaphore_signal(barrier, inc=1, device_id=(dp, other), device_id_type=pl.DeviceIdType.MESH)
    lax.fori_loop(1, n_dp, greet, 0)

    index = [jnp.int32(0)] * SEND_MOST
    target = [jnp.int32(-1)] * SEND_MOST
    count = jnp.int32(0)
    for example in range(selection.shape[0]):
        chosen = selection[example] > 0
        goal = destination[example]
        for k in range(SEND_MOST):
            hit = jnp.logical_and(chosen, count == k)
            index[k] = jnp.where(hit, example, index[k])
            target[k] = jnp.where(hit, goal, target[k])
        count = count + chosen.astype(jnp.int32)

    loads[0].wait()
    for k in range(SEND_MOST):
        pix[k, mp] = pixels_v[index[k]]
    loads[1].wait()
    line = lax.broadcasted_iota(jnp.int32, (32, 16), 0) // 8
    wanted = jnp.where(line == 0, index[0], jnp.where(line == 1, index[1], index[2]))
    chosen_rows = (lax.broadcasted_iota(jnp.int32, (32, 16), 1) == wanted).astype(F32).astype(BF16)
    tiles = diagonal(dot(chosen_rows, captions_v[...]))
    for k in range(SEND_MOST):
        cap_send[k] = tiles[8 * k : 8 * k + 8].astype(BF16)
    lane = lax.broadcasted_iota(jnp.int32, (8, 128), 1)
    goals = jnp.where(lane == 0, target[0], jnp.where(lane == 1, target[1], jnp.where(lane == 2, target[2], -1)))
    cap_send[3] = goals.astype(F32).astype(BF16)
    caps[dp] = cap_send[...]
    loads[3].wait()
    loads[5].wait()

    pl.semaphore_wait(barrier, n_dp - 1 + 3)

    mp_peers = ((right, 0), (left, 1), (opposite, 2))
    mp_sources = ((left, 0), (right, 1), (opposite, 2))
    for other, n in mp_peers:
        send(place.at[mp, core, y], px_s.at[n], px_r.at[n], (dp, other))

    def ring_send(piece, half, sends, receives, to_right, to_left):
        send(piece, sends.at[0], receives.at[0], to_right)
        send(piece, sends.at[1], receives.at[1], to_left)

    def ring_forward(from_left, from_right, half, sends, receives, to_right, to_left, lead=()):
        arrival(from_left, receives.at[0])
        first = from_left.at[pl.ds(0, half)]
        send(first, sends.at[2], receives.at[2], to_right)
        arrival(from_right, receives.at[1])
        second = from_right.at[pl.ds(half, half)]
        send(second, sends.at[3], receives.at[3], to_left)

    def ring_finish(far, half, receives):
        arrival(far.at[pl.ds(0, half)], receives.at[2])
        arrival(far.at[pl.ds(half, half)], receives.at[3])

    to_right, to_left = (dp, right), (dp, left)
    slice_rows = wo.shape[3]
    patch_rows = pix.shape[2]
    rows = n_mp * patch_rows

    def pix_send(k):
        ring_send(pix.at[k, mp], patch_rows // 2, pix_s.at[k], pix_r.at[k], to_right, to_left)

    def pix_forward(k):
        ring_forward(
            pix.at[k, left], pix.at[k, right], patch_rows // 2, pix_s.at[k], pix_r.at[k], to_right, to_left
        )

    ring_send(wo.at[mp, core, y], slice_rows // 2, wx_s, wx_r, to_right, to_left)
    pix_send(0)
    for source, n in mp_sources:
        arrival(place.at[source, core, y], px_r.at[n])
        for step in range(1, Y):
            send(
                place.at[source, core, y], py_s.at[n, step - 1], py_r.at[n, step - 1], (on_y(step), mp)
            )
    ring_forward(
        wo.at[left, core, y], wo.at[right, core, y], slice_rows // 2, wx_s, wx_r, to_right, to_left
    )
    pix_send(1)
    pix_forward(0)
    pix_send(2)
    for source, n in mp_sources:
        for step in range(1, Y):
            arrival(place.at[source, core, (y + Y - step) % Y], py_r.at[n, step - 1])
        send(place.at[source, core], pc_s.at[n], pc_r.at[n], (partner, mp))
    ring_finish(wo.at[opposite, core, y], slice_rows // 2, wx_r)
    for source, n in mp_sources:
        ring_send(
            wo.at[source, core, y], slice_rows // 2, wy_s.at[n], wy_r.at[n], (on_y(1), mp), (on_y(Y - 1), mp)
        )

    def cast_captions(step, carry):
        remote(cap_send, caps.at[dp], cap_s, cap_r, ((dp + step) % n_dp, mp)).start()
        return carry

    lax.fori_loop(1, n_dp, cast_captions, 0)
    pix_forward(1)
    loads[2].wait()
    for source, n in mp_sources:
        arrival(place.at[source, 1 - core], pc_r.at[n])
    loads[4].wait()

    gain0, gain1 = gains[0:1, :], gains[1:2, :]
    width = gains.shape[1]
    chunk_rows = 32

    def norm_into(k, gain):
        def one(part, carry):
            span = pl.ds(pl.multiple_of(part * chunk_rows, chunk_rows), chunk_rows)
            normed[span, :] = norm_rows(hid[k, span, :], gain).astype(BF16)
            return carry

        lax.fori_loop(0, rows // chunk_rows, one, 0, unroll=2)

    half_lane = lax.broadcasted_iota(jnp.int32, (rows, 128), 1) < HEAD_DIM
    ones = jnp.ones((rows, 128), BF16)
    to_both = (to_right, to_left)

    def attend(k, carry):
        ring_finish(pix.at[k, opposite], patch_rows // 2, pix_r.at[k])
        image = pix[k].reshape(rows, pix.shape[3])
        hid[k] = dot(image, patch_v[...]) + place[...].astype(F32).reshape(rows, width)
        norm_into(k, gain0)
        qkv[0] = (dot(normed[...], qkv_v[0]).astype(BF16) * BF16(HEAD_DIM ** (-0.5))).astype(BF16)
        qkv[1] = dot(normed[...], qkv_v[1]).astype(BF16)
        qkv[2] = dot(normed[...], qkv_v[2]).astype(BF16)
        for pair in range(qkv.shape[2] // 128):
            span = slice(pair * 128, pair * 128 + 128)
            query, keys, values = qkv[0, :, span], qkv[1, :, span], qkv[2, :, span]
            widened = jnp.concatenate([values, ones], axis=1)
            outs = []
            for head in range(2):
                mask = half_lane if head == 0 else jnp.logical_not(half_lane)
                mine = jnp.where(mask, query, jnp.zeros_like(query))
                scores = lax.dot_general(mine, keys, NT, preferred_element_type=F32)
                raised = jnp.exp(scores - jnp.max(scores, axis=1, keepdims=True)).astype(BF16)
                both = dot(raised, widened)
                outs.append(both[:, :128] / both[:, 128:])
            ctx[k, mp, :, span] = jnp.where(half_lane, outs[0], outs[1]).astype(BF16)
        for n, where in enumerate(to_both):
            remote(ctx.at[k, mp], ctx.at[k, mp], ctx_s.at[k, n], ctx_r.at[k, n], where).start()
        return carry

    attend(0, 0)
    pix_forward(2)
    for source, n in mp_sources:
        ring_forward(
            wo.at[source, core, y_down], wo.at[source, core, y_up], slice_rows // 2, wy_s.at[n], wy_r.at[n],
            (on_y(1), mp), (on_y(Y - 1), mp),
        )
    lax.fori_loop(1, SEND_MOST, attend, 0)
    for source, n in mp_sources:
        ring_finish(wo.at[source, core, y_far], slice_rows // 2, wy_r.at[n])
        send(wo.at[source, core], wc_s.at[n], wc_r.at[n], (partner, mp))
    half = rows // 2

    def ctx_forward(k):
        ring_forward(ctx.at[k, left], ctx.at[k, right], half, ctx_s.at[k], ctx_r.at[k], to_right, to_left)

    ctx_forward(0)

    others = caps.at[pl.ds(0, n_dp - 1)]
    pltpu.make_async_copy(others, others, cap_r).wait()
    flat = n_dp * 8
    goals = caps[:, 3].astype(F32).reshape(flat, 128)
    here = goals == dp.astype(F32)
    match = jnp.where(here, 1.0, 0.0)
    present = jnp.broadcast_to(jnp.sum(match, axis=1, keepdims=True), (flat, 128))
    row, column = (lax.broadcasted_iota(jnp.int32, (flat, flat), n) for n in range(2))
    earlier = jnp.where(jnp.logical_and(row // 8 > column // 8, column % 8 == 0), 1.0, 0.0).astype(BF16)
    order = dot(earlier, present.astype(BF16))
    lane = lax.broadcasted_iota(jnp.int32, (flat, 128), 1)
    line = lax.broadcasted_iota(jnp.int32, (flat, 128), 0)
    in_slot = jnp.where(order == (lane % 4).astype(F32), present, 0.0)
    spread = jnp.where(jnp.logical_and(line % 8 == lane // 16, lane % 16 < 12), in_slot, 0.0)
    picker[...] = spread.T.astype(BF16)
    filled = jnp.sum(jnp.max(in_slot.reshape(n_dp, 8, 128), axis=1), axis=0, keepdims=True)
    scale = 10.0 * jnp.exp(jnp.full((1, 128), loss_params[0], F32))
    shift = 2.0 * jnp.full((1, 128), loss_params[1], F32)
    for k in range(SEND_MOST):
        tiles = caps[:, k].astype(F32)
        caps_flat[pl.ds(k * flat, flat), :] = tiles.reshape(flat, 128).astype(BF16)
        square = jnp.sum(jnp.sum(tiles * tiles, axis=1), axis=1, keepdims=True)
        length = lax.rsqrt(square / width + EPS) * width ** (-0.5)
        weight_of[k] = length * scale
        column_of = jnp.sum(jnp.where(lane == k, match, 0.0), axis=1, keepdims=True)
        same = jnp.max((column_of * in_slot).reshape(n_dp, 8, 128), axis=1)
        alive = jnp.max(jnp.where(lane == k, goals, -1.0), axis=1, keepdims=True)
        alive = jnp.max(jnp.broadcast_to(alive, (flat, 128)).reshape(n_dp, 8, 128), axis=1)
        sign_of[k] = jnp.where(alive >= 0.0, 1.0 - 2.0 * same, 0.0)

    ctx_forward(1)
    ctx_forward(2)
    for source, n in mp_sources:
        arrival(wo.at[source, 1 - core], wc_r.at[n])
    loads[6].wait()

    def expand(k, carry):
        ring_finish(ctx.at[k, opposite], half, ctx_r.at[k])
        context = jnp.concatenate([ctx[k, source] for source in range(n_mp)], axis=1)
        hid[k] = hid[k] + dot(context, wo[...].reshape(width, width))
        norm_into(k, gain1)
        own = jnp.sum(hid[k, pl.ds(pl.multiple_of(mp * patch_rows, patch_rows), patch_rows), :], axis=0, keepdims=True)
        shared[mp, k] = diagonal(jnp.broadcast_to(own, (8, width)))
        block = 256
        for n in range(up_v.shape[1] // block):
            span = slice(n * block, n * block + block)
            units = jax.nn.gelu(dot(normed[...], up_v[:, span]))
            total = jnp.sum(units, axis=0, keepdims=True)
            summed[k, :, span] = jnp.broadcast_to(total, (8, block))
        return carry

    lax.fori_loop(0, SEND_MOST, expand, 0)

    loads[7].wait()
    totals = summed[...].reshape(SEND_MOST * 8, width)
    high = totals.astype(BF16)
    low = (totals - high.astype(F32)).astype(BF16)
    down = dot(high, down_v[...]) + dot(low, down_v[...])
    shared[mp] = shared[mp] + diagonal(down).reshape(SEND_MOST, 8, 128)
    for other, n in mp_peers:
        send(shared.at[mp], ar_s.at[n], ar_r.at[n], (dp, other))
    for source, n in mp_sources:
        arrival(shared.at[source], ar_r.at[n])
    pooled = (shared[0] + shared[1]) + (shared[2] + shared[3])
    pooled = pooled / rows

    def mean_of(tiles):
        return jnp.sum(jnp.sum(tiles, axis=2, keepdims=True), axis=1, keepdims=True) / width

    centred = pooled - mean_of(pooled)
    gain2 = diagonal(jnp.broadcast_to(gains[2:3, :], (8, width)))
    ready = centred * lax.rsqrt(mean_of(centred * centred) + EPS) * gain2[None]
    goal_of = lax.broadcasted_iota(jnp.int32, (n_dp, 8, 128), 0)
    outgoing = jnp.zeros((n_dp, 8, 128), F32)
    for k in range(SEND_MOST):
        outgoing = jnp.where(goal_of == target[k], ready[k][None], outgoing)
    out_send[...] = outgoing.astype(BF16)
    arrived[dp] = out_send[dp]

    def deliver(step, carry):
        there = (dp + step) % n_dp
        remote(out_send.at[there], arrived.at[dp], out_s, out_r, (there, mp)).start()
        return carry

    lax.fori_loop(1, n_dp, deliver, 0)
    loads[8].wait()
    others = arrived.at[pl.ds(0, n_dp - 1)]
    pltpu.make_async_copy(others, others, out_r).wait()

    slots = dot(picker[...], arrived[...].astype(F32).reshape(flat, 128).astype(BF16)).astype(BF16)
    slots = jnp.concatenate([slots[n * 16 : n * 16 + 16] for n in range(8)], axis=1)
    embedded = dot(slots, embedding_v[...])
    embedded_out[...] = embedded[:RECV_MOST]
    unit = embedded * (lax.rsqrt(jnp.mean(embedded * embedded, axis=1, keepdims=True) + EPS) * width ** (-0.5))
    first = unit.astype(BF16).astype(F32)
    rest = unit - first
    second = rest.astype(BF16).astype(F32)
    line = lax.broadcasted_iota(jnp.int32, unit.shape, 0)
    parts = jnp.where(line < 4, first, jnp.where(line < 8, second, jnp.where(line < 12, rest - second, 0.0)))
    parts = parts.astype(BF16)
    parts = jnp.concatenate([parts[:, n * 128 : n * 128 + 128] for n in range(8)], axis=0)
    products = lax.dot_general(caps_flat[...], parts, NT, preferred_element_type=F32)
    line = lax.broadcasted_iota(jnp.int32, (SEND_MOST * flat, 128), 0)
    lane = lax.broadcasted_iota(jnp.int32, (SEND_MOST * flat, 128), 1)
    products = jnp.where(line % 8 == lane // 16, products, 0.0).reshape(SEND_MOST * n_dp, 8, 128)
    products = jnp.sum(products, axis=1)
    for step in (64, 32, 16, 8, 4):
        products = products + pltpu.roll(products, step, 1)
    weights = weight_of[...].reshape(SEND_MOST * n_dp, 128)
    signs = sign_of[...].reshape(SEND_MOST * n_dp, 128)
    terms = signs * (products * weights + shift)
    terms = jnp.maximum(terms, 0.0) + jnp.log1p(jnp.exp(-jnp.abs(terms)))
    terms = jnp.where(signs == 0.0, 0.0, terms)
    losses = jnp.sum(terms, axis=0, keepdims=True) / float(n_dp * SEL_DEV)
    losses_out[...] = jnp.where(filled > 0.0, losses, 0.0)

    for src, ref, sends, receives, where in pending:
        remote(src, ref, sends, receives, where).wait_send()
    for k in range(SEND_MOST):
        for n, where in enumerate(to_both):
            remote(ctx.at[k, mp], ctx.at[k, mp], ctx_s.at[k, n], ctx_r.at[k, n], where).wait_send()
    others = caps.at[pl.ds(0, n_dp - 1)]
    pltpu.make_async_copy(others, others, cap_s).wait()
    others = arrived.at[pl.ds(0, n_dp - 1)]
    pltpu.make_async_copy(others, others, out_s).wait()


def per_device(
    pixels, selection, destination, patch_weight, position, query_key_value, output_weight, up_weight,
    down_weight, norm_gains, embedding_weight, caption_vectors, loss_params,
):
    n_dp, n_mp = lax.axis_size("dp"), lax.axis_size("mp")
    width, units = up_weight.shape
    share = query_key_value.shape[2]
    patch_rows, values = pixels.shape[1:]
    rows = n_mp * patch_rows
    place_rows = position.shape[0] // (Y * CORES)
    slice_rows = output_weight.shape[0] // (Y * CORES)
    position = position.reshape(CORES, Y, place_rows, width)
    output_weight = output_weight.reshape(CORES, Y, slice_rows, width)
    smem = pl.BlockSpec(memory_space=pltpu.SMEM)
    vmem = pl.BlockSpec(memory_space=pltpu.VMEM)
    far = pl.BlockSpec(memory_space=pl.ANY)
    dma = pltpu.SemaphoreType.DMA
    n = SEND_MOST
    scratch = [
        pltpu.VMEM(pixels.shape, BF16), pltpu.VMEM(patch_weight.shape, BF16),
        pltpu.VMEM(query_key_value.shape, BF16), pltpu.VMEM(up_weight.shape, BF16),
        pltpu.VMEM(down_weight.shape, BF16), pltpu.VMEM(embedding_weight.shape, BF16),
        pltpu.VMEM(caption_vectors.shape, BF16),
        pltpu.VMEM((n, n_mp, patch_rows, values), BF16),
        pltpu.VMEM((n_mp, CORES, Y, place_rows, width), BF16),
        pltpu.VMEM((n_mp, CORES, Y, slice_rows, width), BF16),
        pltpu.VMEM((n, rows, width), F32), pltpu.VMEM((rows, width), BF16),
        pltpu.VMEM((3, rows, share), BF16), pltpu.VMEM((n, n_mp, rows, share), BF16),
        pltpu.VMEM((n + 1, 8, 128), BF16), pltpu.VMEM((n_dp, n + 1, 8, 128), BF16),
        pltpu.VMEM((n * n_dp * 8, 128), BF16), pltpu.VMEM((n, 8, units), F32),
        pltpu.VMEM((n_mp, n, 8, 128), F32),
        pltpu.VMEM((n_dp, 8, 128), BF16), pltpu.VMEM((n_dp, 8, 128), BF16),
        pltpu.VMEM((128, n_dp * 8), BF16), pltpu.VMEM((n, n_dp, 128), F32), pltpu.VMEM((n, n_dp, 128), F32),
        dma((9,)), dma((n, 4)), dma((n, 4)), dma((3,)), dma((3,)), dma((3, 3)), dma((3, 3)), dma((3,)), dma((3,)),
        dma((4,)), dma((4,)), dma((3, 4)), dma((3, 4)), dma((3,)), dma((3,)),
        dma((n, 4)), dma((n, 4)), dma((3,)), dma((3,)), dma, dma, dma, dma,
    ]
    embedded, losses = pl.pallas_call(
        functools.partial(body, n_dp, n_mp),
        out_shape=(
            jax.ShapeDtypeStruct((RECV_MOST, width), F32),
            jax.ShapeDtypeStruct((1, 128), F32),
        ),
        in_specs=[smem, smem, smem, far, far, far, far, far, far, far, vmem, far, far],
        out_specs=(vmem, vmem),
        scratch_shapes=scratch,
        name="learner",
        compiler_params=pltpu.CompilerParams(
            collective_id=0, has_side_effects=True, vmem_limit_bytes=60 * 1024 * 1024
        ),
    )(
        selection, destination, loss_params, pixels, patch_weight, position, query_key_value, output_weight,
        up_weight, down_weight, norm_gains, embedding_weight, caption_vectors,
    )
    return embedded, losses[0, :RECV_MOST]


def solution(mesh):
    in_specs = (
        P("dp", "mp", None), P("dp"), P("dp"), P(), P("mp", None), P(None, None, "mp"), P("mp", None),
        P(None, "mp"), P("mp", None), P(), P(), P("dp", None), P(),
    )
    out_specs = (P("dp", None), P("dp"))
    return jax.shard_map(per_device, mesh=mesh, in_specs=in_specs, out_specs=out_specs, check_vma=False)
```

time: 189 us -> 67.7 us (0.36)
  blocking collectives: 93.9 us -> 0 us
  Pallas kernels: 0 us -> 64.3 us
  waiting for transfers between devices: 24.9 us -> 0 us
  between operations: 22 us -> 0.64 us
  matrix products: 21.3 us -> 0 us
  starting transfers between devices: 10.2 us -> 0 us
  local copies, waits for them, and re-layouts: 9.66 us -> 2.46 us
  other arithmetic: 6.19 us -> 0 us
    all_gather x3 -> x0, blocking collectives: 73.5 us -> none  [the longest x1 52.1 us: per_device(): all_captions = lax.all_gather(captions, 'dp', axis=0, tiled=True)]
    pallas_call x0 -> x1, Pallas kernels: none -> 64.3 us  [per_device(): pl.pallas_call(functools.partial(body, n_dp, n_mp), out_shape=(jax.ShapeD...]
    unnamed x1 -> x0, blocking collectives: 20.4 us -> none
    dot_general x10 -> x0, matrix products: 18.4 us -> none  [the longest x1 5.1 us: per_device(): jnp.einsum('mrpk,mkd->rpd', context, segments, preferred_element_type=f32)]
    all_gather x3 -> x0, waiting for transfers between devices: 15.3 us -> none  [the longest x1 15.3 us: per_device(): image = lax.all_gather(image, 'mp', axis=1, tiled=True)]
    all_to_all x1 -> x0, starting transfers between devices: 10 us -> none  [per_device(): lax.all_to_all(outgoing, 'dp', split_axis=0, concat_axis=0, tiled=True)]
    all_to_all x1 -> x0, waiting for transfers between devices: 8.89 us -> none  [per_device(): lax.all_to_all(outgoing, 'dp', split_axis=0, concat_axis=0, tiled=True)]
    unnamed x26 -> x1, local copies, waits for them, and re-layouts: 4.33 us -> 1.32 us
  transfers between devices with their start and end apart: 4 -> 0, of which waited for: 2 -> 0; matrix products, arithmetic and copies ran while one was open for 8% -> 0% of each run, Pallas kernels for 0% -> 0%
where the time goes in v2:
time: 67.7 us; the launch traced here: 67.4 us
  Pallas kernels  64.3 us (95%)
  local copies, waits for them, and re-layouts  2.46 us (4%)
    pallas_call x1, Pallas kernels, per_device(): pl.pallas_call(functools.partial(body, n_dp, n_mp), out_shape=(jax.ShapeD...  64.3 us

profile of v2, /device:TPU:1, one launch (start us, length us, event | category | flops | bytes accessed | tf_op | source)
XLA Modules:
  0.0 67.4 jit_solution(4011612012008215473)
XLA Ops:
  0.6 64.3 %learner.1 = (f32[4,1024]{1,0:T(4,128)}, f32[1,128]{1,0:T(1,128)}) custom-call(s32[16]{0:T(128)} %selection.1, s32[16]{0:T(128)} %destination.1, f32[2]{0:T(128)} %loss_params.1, bf16[16,64,768]{2,1,0:T(8,128)(2,1)} %pixels.1, bf16[768,1024]{1,0:T(8,128)(2,1)} %patch_weight.1, bf16[2,4,8,1024]{3,2,1,0:T(8,128)(2,1)} %bitcast.5, ...), custom_call_target="tpu_custom_call" | custom-call | tf_op jit(solution)/shard_map/learner/pallas_call | solution.py:419
  64.9 1.1 %slice_bitcast_fusion = f32[4]{0:T(128)} fusion(f32[1,128]{1,0:T(1,128)} %get-tuple-element.5), kind=kLoop, calls=%fused_computation | loop fusion | bytes 32 | tf_op jit(solution)/shard_map/squeeze | solution.py:436
  66.0 1.3 %copy.16 = f32[4,1024]{1,0:T(4,128)} copy(f32[4,1024]{1,0:T(4,128)} %get-tuple-element.8) | data formatting | bytes 32768

commit v3 on v2

v3 whole, which is shorter than its diff:
```python
import functools

import jax
import jax.numpy as jnp
from jax import lax
from jax.experimental import pallas as pl
from jax.experimental.pallas import tpu as pltpu
from jax.sharding import PartitionSpec as P

EPS = 1e-06
SEND_MOST = 3
RECV_MOST = 4
SEL_DEV = 2
HEAD_DIM = 64
Y, CORES = 4, 2
F32, BF16 = jnp.float32, jnp.bfloat16
NT = (((1,), (1,)), ((), ()))


def norm_rows(values, gain):
    center = jnp.mean(values, axis=-1, keepdims=True)
    centred = values - center
    spread = jnp.mean(centred * centred, axis=-1, keepdims=True)
    return centred * lax.rsqrt(spread + EPS) * gain


def diagonal(rows):
    count = rows.shape[0]
    line = lax.broadcasted_iota(jnp.int32, (count, 128), 0) % 8
    out = jnp.zeros((count, 128), rows.dtype)
    for chunk in range(8):
        out = jnp.where(line == chunk, rows[:, chunk * 128 : (chunk + 1) * 128], out)
    return out


def dot(a, b):
    return jnp.dot(a, b, preferred_element_type=F32)


def body(
    n_dp, n_mp,
    selection_h, destination_h, loss_params_h, pixels, patch_weight, position, query_key_value, output_weight,
    up_weight, down_weight, gains_h, embedding_weight, captions,
    embedded_out, losses_out,
    selection, destination, loss_params, gains, pixels_v, patch_v, qkv_v, up_v, down_v, embedding_v, captions_v,
    pix, place, wo, hid, normed, qkv, ctx, cap_send, caps, caps_flat, summed, shared,
    out_send, arrived, picker, sign_of, weight_of,
    local, pix_s, pix_r, px_s, px_r, py_s, py_r, pc_s, pc_r, wx_s, wx_r, wy_s, wy_r, wc_s, wc_r,
    ctx_s, ctx_r, ar_s, ar_r, cy_s, cy_r, cz_s, cz_r, cc_s, cc_r, out_s, out_r, entered,
):
    dp, mp = lax.axis_index("dp"), lax.axis_index("mp")
    right, left, opposite = (mp + 1) % n_mp, (mp + n_mp - 1) % n_mp, (mp + 2) % n_mp
    core, y, z = dp % CORES, (dp // CORES) % Y, dp // (CORES * Y)

    def on_y(step):
        return (z * Y + (y + step) % Y) * CORES + core

    partner = dp + 1 - 2 * core

    def remote(src, dst, sends, receives, where):
        return pltpu.make_async_remote_copy(
            src_ref=src, dst_ref=dst, send_sem=sends, recv_sem=receives, device_id=where,
            device_id_type=pl.DeviceIdType.MESH,
        )

    draining = []

    def arrival(ref, receives):
        if draining:
            return
        remote(ref, ref, receives, receives, (dp, right)).wait_recv()

    def send(ref, sends, receives, where):
        copy = remote(ref, ref, sends, receives, where)
        if draining:
            copy.wait_send()
        else:
            copy.start()

    barrier = pltpu.get_barrier_semaphore()

    def greet(where):
        pl.semaphore_signal(barrier, inc=1, device_id=where, device_id_type=pl.DeviceIdType.MESH)

    def far_first(act):
        act(dp, n_dp // 2)

        def both(step, carry):
            act(dp, n_dp // 2 - step)
            act(dp, n_dp // 2 + step)
            return carry

        lax.fori_loop(1, n_dp // 2, both, 0)

    loads = [
        (selection_h, selection), (destination_h, destination), (pixels, pixels_v), (captions, captions_v),
        (position, place.at[mp]), (output_weight, wo.at[mp]), (patch_weight, patch_v), (gains_h, gains),
        (query_key_value, qkv_v), (loss_params_h, loss_params), (up_weight, up_v), (down_weight, down_v),
        (embedding_weight, embedding_v),
    ]
    loads = [pltpu.make_async_copy(a, b, local.at[n]) for n, (a, b) in enumerate(loads)]
    for load in loads[:4]:
        load.start()
    near = [(dp, opposite), (on_y(2), mp), (dp, right), (dp, left), (on_y(1), mp), (on_y(Y - 1), mp), (partner, mp)]
    n_z = n_dp // (Y * CORES)
    z_near = [((dp + step * Y * CORES) % n_dp, mp) for step in (1, n_z - 1)] if n_z > 1 else []
    for where in near + z_near:
        greet(where)
    for load in loads[4:]:
        load.start()

    loads[0].wait()
    loads[1].wait()
    index = [jnp.int32(0)] * SEND_MOST
    target = [jnp.int32(-1)] * SEND_MOST
    count = jnp.int32(0)
    for example in range(selection.shape[0]):
        chosen = selection[example] > 0
        goal = destination[example]
        for k in range(SEND_MOST):
            hit = jnp.logical_and(chosen, count == k)
            index[k] = jnp.where(hit, example, index[k])
            target[k] = jnp.where(hit, goal, target[k])
        count = count + chosen.astype(jnp.int32)

    loads[2].wait()
    for k in range(SEND_MOST):
        pix[k, mp] = pixels_v[index[k]]
    loads[3].wait()
    line = lax.broadcasted_iota(jnp.int32, (32, 16), 0) // 8
    wanted = jnp.where(line == 0, index[0], jnp.where(line == 1, index[1], index[2]))
    chosen_rows = (lax.broadcasted_iota(jnp.int32, (32, 16), 1) == wanted).astype(F32).astype(BF16)
    tiles = diagonal(dot(chosen_rows, captions_v[...]))
    for k in range(SEND_MOST):
        cap_send[k] = tiles[8 * k : 8 * k + 8].astype(BF16)
    lane = lax.broadcasted_iota(jnp.int32, (8, 128), 1)
    goals = jnp.where(lane == 0, target[0], jnp.where(lane == 1, target[1], jnp.where(lane == 2, target[2], -1)))
    cap_send[3] = goals.astype(F32).astype(BF16)
    caps[core, z, y] = cap_send[...]
    loads[4].wait()
    loads[5].wait()

    pl.semaphore_wait(barrier, len(near + z_near))

    def tell(step):
        for where in z_near if step else [(on_y(n), mp) for n in range(1, Y)]:
            pl.semaphore_signal(entered.at[step], inc=1, device_id=where, device_id_type=pl.DeviceIdType.MESH)

    def told(step):
        pl.semaphore_wait(entered.at[step], len(z_near) if step else Y - 1)

    tell(0)

    mp_peers = ((right, 0), (left, 1), (opposite, 2))
    mp_sources = ((left, 0), (right, 1), (opposite, 2))

    def halves(piece):
        half = piece.shape[0] // 2
        return piece.at[pl.ds(0, half)], piece.at[pl.ds(half, half)]

    def ring_send(piece, sends, receives, to_right, to_left):
        first, second = halves(piece)
        send(first, sends.at[0], receives.at[0], to_right)
        send(second, sends.at[2], receives.at[2], to_left)
        send(second, sends.at[1], receives.at[1], to_right)
        send(first, sends.at[3], receives.at[3], to_left)

    def ring_forward(from_left, from_right, sends, receives, to_right, to_left):
        first, second = halves(from_left)[0], halves(from_right)[1]
        arrival(first, receives.at[0])
        send(first, sends.at[4], receives.at[4], to_right)
        arrival(second, receives.at[2])
        send(second, sends.at[5], receives.at[5], to_left)

    def ring_finish(from_left, from_right, far, receives):
        arrival(halves(from_left)[1], receives.at[1])
        arrival(halves(from_right)[0], receives.at[3])
        arrival(halves(far)[0], receives.at[4])
        arrival(halves(far)[1], receives.at[5])

    to_right, to_left = (dp, right), (dp, left)
    patch_rows = pix.shape[2]
    rows = n_mp * patch_rows

    def pix_send(k):
        ring_send(pix.at[k, mp], pix_s.at[k], pix_r.at[k], to_right, to_left)

    def pix_forward(k):
        ring_forward(
            pix.at[k, left], pix.at[k, right], pix_s.at[k], pix_r.at[k], to_right, to_left
        )

    def place_x():
        for other, n in mp_peers:
            send(place.at[mp, core, y], px_s.at[n], px_r.at[n], (dp, other))

    def place_y():
        for source, n in mp_sources:
            arrival(place.at[source, core, y], px_r.at[n])
            for step in range(1, Y):
                send(
                    place.at[source, core, y], py_s.at[n, step - 1], py_r.at[n, step - 1], (on_y(step), mp)
                )

    def place_core():
        for source, n in mp_sources:
            for step in range(1, Y):
                arrival(place.at[source, core, (y + Y - step) % Y], py_r.at[n, step - 1])
            send(place.at[source, core], pc_s.at[n], pc_r.at[n], (partner, mp))

    def wo_x():
        ring_send(wo.at[mp, core, y], wx_s, wx_r, to_right, to_left)

    def wo_x_forward():
        ring_forward(wo.at[left, core, y], wo.at[right, core, y], wx_s, wx_r, to_right, to_left)

    def wo_y():
        ring_finish(wo.at[left, core, y], wo.at[right, core, y], wo.at[opposite, core, y], wx_r)
        for source, n in mp_sources:
            for step in (2, 1, 3):
                send(wo.at[source, core, y], wy_s.at[n, step - 1], wy_r.at[n, step - 1], (on_y(step), mp))

    def wo_core():
        for source, n in mp_sources:
            for step in range(1, Y):
                arrival(wo.at[source, core, (y + Y - step) % Y], wy_r.at[n, step - 1])
            send(wo.at[source, core], wc_s.at[n], wc_r.at[n], (partner, mp))

    def caps_y():
        for step in range(1, Y):
            send(caps.at[core, z, y], cy_s.at[step - 1], cy_r.at[step - 1], (on_y(step), mp))

    def caps_z():
        for step in range(1, Y):
            arrival(caps.at[core, z, (y + Y - step) % Y], cy_r.at[step - 1])
        for step in range(1, n_z):
            there = ((((z + step) % n_z) * Y + y) * CORES + core, mp)
            send(caps.at[core, z], cz_s.at[step - 1], cz_r.at[step - 1], there)

    def caps_core():
        for step in range(1, n_z):
            arrival(caps.at[core, (z + n_z - step) % n_z], cz_r.at[step - 1])
        send(caps.at[core], cc_s, cc_r, (partner, mp))

    place_x()
    pix_send(0)
    wo_x()
    caps_y()
    place_y()
    pix_send(1)
    told(0)
    tell(1)
    pix_forward(0)
    wo_x_forward()
    pix_send(2)
    told(1)
    tell(2)
    place_core()
    told(2)
    tell(3)
    pix_forward(1)
    loads[6].wait()
    loads[7].wait()
    loads[8].wait()

    gain0, gain1 = gains[0:1, :], gains[1:2, :]
    width = gains.shape[1]
    chunk_rows = 32

    def norm_into(k, gain):
        def one(part, carry):
            span = pl.ds(pl.multiple_of(part * chunk_rows, chunk_rows), chunk_rows)
            normed[span, :] = norm_rows(hid[k, span, :], gain).astype(BF16)
            return carry

        lax.fori_loop(0, rows // chunk_rows, one, 0, unroll=2)

    half_lane = lax.broadcasted_iota(jnp.int32, (rows, 128), 1) < HEAD_DIM
    ones = jnp.ones((rows, 128), BF16)

    def ctx_send(k):
        ring_send(ctx.at[k, mp], ctx_s.at[k], ctx_r.at[k], to_right, to_left)

    def ctx_forward(k):
        ring_forward(ctx.at[k, left], ctx.at[k, right], ctx_s.at[k], ctx_r.at[k], to_right, to_left)

    def attend(k, carry):
        ring_finish(pix.at[k, left], pix.at[k, right], pix.at[k, opposite], pix_r.at[k])
        image = pix[k].reshape(rows, pix.shape[3])
        hid[k] = dot(image, patch_v[...])

        @pl.when(k == 0)
        def _():
            for source, n in mp_sources:
                arrival(place.at[source, 1 - core], pc_r.at[n])
            told(3)
            tell(4)
            wo_y()

        hid[k] = hid[k] + place[...].astype(F32).reshape(rows, width)
        norm_into(k, gain0)
        qkv[0] = (dot(normed[...], qkv_v[0]).astype(BF16) * BF16(HEAD_DIM ** (-0.5))).astype(BF16)
        qkv[1] = dot(normed[...], qkv_v[1]).astype(BF16)
        qkv[2] = dot(normed[...], qkv_v[2]).astype(BF16)
        @pl.when(k == 2)
        def _():
            caps_core()

        for pair in range(qkv.shape[2] // 128):
            span = slice(pair * 128, pair * 128 + 128)
            query, keys, values = qkv[0, :, span], qkv[1, :, span], qkv[2, :, span]
            widened = jnp.concatenate([values, ones], axis=1)
            outs = []
            for head in range(2):
                mask = half_lane if head == 0 else jnp.logical_not(half_lane)
                mine = jnp.where(mask, query, jnp.zeros_like(query))
                scores = lax.dot_general(mine, keys, NT, preferred_element_type=F32)
                raised = jnp.exp(scores - jnp.max(scores, axis=1, keepdims=True)).astype(BF16)
                both = dot(raised, widened)
                outs.append(both[:, :128] / both[:, 128:])
            ctx[k, mp, :, span] = jnp.where(half_lane, outs[0], outs[1]).astype(BF16)

        ctx_send(k)

        @pl.when(k == 0)
        def _():
            pix_forward(2)
            told(4)
            caps_z()

        @pl.when(k == 1)
        def _():
            ctx_forward(0)

        return carry

    lax.fori_loop(0, SEND_MOST, attend, 0)
    ctx_forward(1)
    wo_core()

    arrival(caps.at[1 - core], cc_r)
    caps_all = caps[...].reshape(n_dp, SEND_MOST + 1, 8, 128)
    flat = n_dp * 8
    goals = caps_all[:, 3].astype(F32).reshape(flat, 128)
    here = goals == dp.astype(F32)
    match = jnp.where(here, 1.0, 0.0)
    present = jnp.broadcast_to(jnp.sum(match, axis=1, keepdims=True), (flat, 128))
    row, column = (lax.broadcasted_iota(jnp.int32, (flat, flat), n) for n in range(2))
    row_dp, column_dp = (n // 8 % (n_dp // CORES) * CORES + n // 8 // (n_dp // CORES) for n in (row, column))
    earlier = jnp.where(jnp.logical_and(row_dp > column_dp, column % 8 == 0), 1.0, 0.0).astype(BF16)
    order = dot(earlier, present.astype(BF16))
    lane = lax.broadcasted_iota(jnp.int32, (flat, 128), 1)
    line = lax.broadcasted_iota(jnp.int32, (flat, 128), 0)
    in_slot = jnp.where(order == (lane % 4).astype(F32), present, 0.0)
    spread = jnp.where(jnp.logical_and(line % 8 == lane // 16, lane % 16 < 12), in_slot, 0.0)
    picker[...] = spread.T.astype(BF16)
    filled = jnp.sum(jnp.max(in_slot.reshape(n_dp, 8, 128), axis=1), axis=0, keepdims=True)
    loads[9].wait()
    scale = 10.0 * jnp.exp(jnp.full((1, 128), loss_params[0], F32))
    shift = 2.0 * jnp.full((1, 128), loss_params[1], F32)
    for k in range(SEND_MOST):
        tiles = caps_all[:, k].astype(F32)
        caps_flat[pl.ds(k * flat, flat), :] = tiles.reshape(flat, 128).astype(BF16)
        square = jnp.sum(jnp.sum(tiles * tiles, axis=1), axis=1, keepdims=True)
        length = lax.rsqrt(square / width + EPS) * width ** (-0.5)
        weight_of[k] = length * scale
        column_of = jnp.sum(jnp.where(lane == k, match, 0.0), axis=1, keepdims=True)
        same = jnp.max((column_of * in_slot).reshape(n_dp, 8, 128), axis=1)
        alive = jnp.max(jnp.where(lane == k, goals, -1.0), axis=1, keepdims=True)
        alive = jnp.max(jnp.broadcast_to(alive, (flat, 128)).reshape(n_dp, 8, 128), axis=1)
        sign_of[k] = jnp.where(alive >= 0.0, 1.0 - 2.0 * same, 0.0)

    for source, n in mp_sources:
        arrival(wo.at[source, 1 - core], wc_r.at[n])
    loads[10].wait()

    def expand(k, carry):
        ring_finish(ctx.at[k, left], ctx.at[k, right], ctx.at[k, opposite], ctx_r.at[k])
        context = jnp.concatenate([ctx[k, source] for source in range(n_mp)], axis=1)
        hid[k] = hid[k] + dot(context, wo[...].reshape(width, width))
        norm_into(k, gain1)
        own = jnp.sum(hid[k, pl.ds(pl.multiple_of(mp * patch_rows, patch_rows), patch_rows), :], axis=0, keepdims=True)
        shared[mp, k] = diagonal(jnp.broadcast_to(own, (8, width)))
        block = 256
        for n in range(up_v.shape[1] // block):
            span = slice(n * block, n * block + block)
            units = jax.nn.gelu(dot(normed[...], up_v[:, span]))
            total = jnp.sum(units, axis=0, keepdims=True)
            summed[k, :, span] = jnp.broadcast_to(total, (8, block))

        @pl.when(k == 0)
        def _():
            ctx_forward(2)

        return carry

    lax.fori_loop(0, SEND_MOST, expand, 0)

    loads[11].wait()
    totals = summed[...].reshape(SEND_MOST * 8, width)
    high = totals.astype(BF16)
    low = (totals - high.astype(F32)).astype(BF16)
    down = dot(jnp.concatenate([high, low], axis=0), down_v[...])
    down = down[: SEND_MOST * 8] + down[SEND_MOST * 8 :]
    shared[mp] = shared[mp] + diagonal(down).reshape(SEND_MOST, 8, 128)

    def share():
        for other, n in mp_peers:
            send(shared.at[mp], ar_s.at[n], ar_r.at[n], (dp, other))

    share()
    for source, n in mp_sources:
        arrival(shared.at[source], ar_r.at[n])
    pooled = (shared[0] + shared[1]) + (shared[2] + shared[3])
    pooled = pooled / rows

    def mean_of(tiles):
        return jnp.sum(jnp.sum(tiles, axis=2, keepdims=True), axis=1, keepdims=True) / width

    centred = pooled - mean_of(pooled)
    gain2 = diagonal(jnp.broadcast_to(gains[2:3, :], (8, width)))
    ready = centred * lax.rsqrt(mean_of(centred * centred) + EPS) * gain2[None]
    goal_of = lax.broadcasted_iota(jnp.int32, (n_dp, 8, 128), 0)
    outgoing = jnp.zeros((n_dp, 8, 128), F32)
    for k in range(SEND_MOST):
        outgoing = jnp.where(goal_of == target[k], ready[k][None], outgoing)
    out_send[...] = outgoing.astype(BF16)
    spot = core * (n_dp // CORES) + dp // CORES
    arrived[spot] = out_send[dp]

    def deliver(me, step):
        there = (me + step) % n_dp
        remote(out_send.at[there], arrived.at[spot], out_s, out_r, (there, mp)).start()

    far_first(deliver)
    loads[12].wait()
    others = arrived.at[pl.ds(0, n_dp - 1)]
    pltpu.make_async_copy(others, others, out_r).wait()

    slots = dot(picker[...], arrived[...].astype(F32).reshape(flat, 128).astype(BF16)).astype(BF16)
    slots = jnp.concatenate([slots[n * 16 : n * 16 + 16] for n in range(8)], axis=1)
    embedded = dot(slots, embedding_v[...])
    embedded_out[...] = embedded[:RECV_MOST]
    unit = embedded * (lax.rsqrt(jnp.mean(embedded * embedded, axis=1, keepdims=True) + EPS) * width ** (-0.5))
    first = unit.astype(BF16).astype(F32)
    rest = unit - first
    second = rest.astype(BF16).astype(F32)
    line = lax.broadcasted_iota(jnp.int32, unit.shape, 0)
    parts = jnp.where(line < 4, first, jnp.where(line < 8, second, jnp.where(line < 12, rest - second, 0.0)))
    parts = parts.astype(BF16)
    parts = jnp.concatenate([parts[:, n * 128 : n * 128 + 128] for n in range(8)], axis=0)
    products = lax.dot_general(caps_flat[...], parts, NT, preferred_element_type=F32)
    line = lax.broadcasted_iota(jnp.int32, (SEND_MOST * flat, 128), 0)
    lane = lax.broadcasted_iota(jnp.int32, (SEND_MOST * flat, 128), 1)
    products = jnp.where(line % 8 == lane // 16, products, 0.0).reshape(SEND_MOST * n_dp, 8, 128)
    products = jnp.sum(products, axis=1)
    for step in (64, 32, 16, 8, 4):
        products = products + pltpu.roll(products, step, 1)
    weights = weight_of[...].reshape(SEND_MOST * n_dp, 128)
    signs = sign_of[...].reshape(SEND_MOST * n_dp, 128)
    terms = signs * (products * weights + shift)
    terms = jnp.maximum(terms, 0.0) + jnp.log1p(jnp.exp(-jnp.abs(terms)))
    terms = jnp.where(signs == 0.0, 0.0, terms)
    losses = jnp.sum(terms, axis=0, keepdims=True) / float(n_dp * SEL_DEV)
    losses_out[...] = jnp.where(filled > 0.0, losses, 0.0)

    draining.append(True)
    for act in (place_x, place_y, place_core, wo_x, wo_x_forward, wo_y, wo_core, caps_y, caps_z, caps_core, share):
        act()
    for k in range(SEND_MOST):
        for act in (pix_send, pix_forward, ctx_send, ctx_forward):
            act(k)
    others = arrived.at[pl.ds(0, n_dp - 1)]
    pltpu.make_async_copy(others, others, out_s).wait()


def hand_over(embedded, losses, embedded_out, losses_out):
    embedded_out[...] = embedded[...]
    losses_out[...] = losses[0, :RECV_MOST]


def per_device(
    pixels, selection, destination, patch_weight, position, query_key_value, output_weight, up_weight,
    down_weight, norm_gains, embedding_weight, caption_vectors, loss_params,
):
    n_dp, n_mp = lax.axis_size("dp"), lax.axis_size("mp")
    width, units = up_weight.shape
    share = query_key_value.shape[2]
    patch_rows, values = pixels.shape[1:]
    rows = n_mp * patch_rows
    place_rows = position.shape[0] // (Y * CORES)
    slice_rows = output_weight.shape[0] // (Y * CORES)
    position = position.reshape(CORES, Y, place_rows, width)
    output_weight = output_weight.reshape(CORES, Y, slice_rows, width)
    vmem = pl.BlockSpec(memory_space=pltpu.VMEM)
    far = pl.BlockSpec(memory_space=pl.ANY)
    dma = pltpu.SemaphoreType.DMA
    n = SEND_MOST
    scratch = [
        pltpu.SMEM(selection.shape, jnp.int32), pltpu.SMEM(destination.shape, jnp.int32),
        pltpu.SMEM(loss_params.shape, F32), pltpu.VMEM(norm_gains.shape, F32),
        pltpu.VMEM(pixels.shape, BF16), pltpu.VMEM(patch_weight.shape, BF16),
        pltpu.VMEM(query_key_value.shape, BF16), pltpu.VMEM(up_weight.shape, BF16),
        pltpu.VMEM(down_weight.shape, BF16), pltpu.VMEM(embedding_weight.shape, BF16),
        pltpu.VMEM(caption_vectors.shape, BF16),
        pltpu.VMEM((n, n_mp, patch_rows, values), BF16),
        pltpu.VMEM((n_mp, CORES, Y, place_rows, width), BF16),
        pltpu.VMEM((n_mp, CORES, Y, slice_rows, width), BF16),
        pltpu.VMEM((n, rows, width), F32), pltpu.VMEM((rows, width), BF16),
        pltpu.VMEM((3, rows, share), BF16), pltpu.VMEM((n, n_mp, rows, share), BF16),
        pltpu.VMEM((n + 1, 8, 128), BF16), pltpu.VMEM((CORES, n_dp // (CORES * Y), Y, n + 1, 8, 128), BF16),
        pltpu.VMEM((n * n_dp * 8, 128), BF16), pltpu.VMEM((n, 8, units), F32),
        pltpu.VMEM((n_mp, n, 8, 128), F32),
        pltpu.VMEM((n_dp, 8, 128), BF16), pltpu.VMEM((n_dp, 8, 128), BF16),
        pltpu.VMEM((128, n_dp * 8), BF16), pltpu.VMEM((n, n_dp, 128), F32), pltpu.VMEM((n, n_dp, 128), F32),
        dma((13,)), dma((n, 6)), dma((n, 6)), dma((3,)), dma((3,)), dma((3, 3)), dma((3, 3)), dma((3,)), dma((3,)),
        dma((6,)), dma((6,)), dma((3, 3)), dma((3, 3)), dma((3,)), dma((3,)),
        dma((n, 6)), dma((n, 6)), dma((3,)), dma((3,)), dma((3,)), dma((3,)),
        dma((7,)), dma((7,)), dma, dma, dma, dma, pltpu.SemaphoreType.REGULAR((5,)),
    ]
    embedded, losses = pl.pallas_call(
        functools.partial(body, n_dp, n_mp),
        out_shape=(
            jax.ShapeDtypeStruct((RECV_MOST, width), F32),
            jax.ShapeDtypeStruct((1, 128), F32),
        ),
        in_specs=[far] * 13,
        out_specs=(vmem, vmem),
        scratch_shapes=scratch,
        name="learner",
        compiler_params=pltpu.CompilerParams(
            collective_id=0, has_side_effects=True, vmem_limit_bytes=60 * 1024 * 1024
        ),
    )(
        selection, destination, loss_params, pixels, patch_weight, position, query_key_value, output_weight,
        up_weight, down_weight, norm_gains, embedding_weight, caption_vectors,
    )
    return pl.pallas_call(
        hand_over,
        out_shape=(jax.ShapeDtypeStruct((RECV_MOST, width), F32), jax.ShapeDtypeStruct((RECV_MOST,), F32)),
        name="hand_over",
    )(embedded, losses)


def solution(mesh):
    in_specs = (
        P("dp", "mp", None), P("dp"), P("dp"), P(), P("mp", None), P(None, None, "mp"), P("mp", None),
        P(None, "mp"), P("mp", None), P(), P(), P("dp", None), P(),
    )
    out_specs = (P("dp", None), P("dp"))
    return jax.shard_map(per_device, mesh=mesh, in_specs=in_specs, out_specs=out_specs, check_vma=False)
```

time: 67.7 us -> 59.2 us (0.87)
  Pallas kernels: 64.3 us -> 58.4 us
  local copies, waits for them, and re-layouts: 2.46 us -> 0 us
    pallas_call x1, Pallas kernels: 64.3 us -> 57.1 us  [per_device(): pl.pallas_call(functools.partial(body, n_dp, n_mp), out_shape=(jax.ShapeD...]
    pallas_call x0 -> x1, Pallas kernels: none -> 1.33 us  [per_device(): pl.pallas_call(hand_over, out_shape=(jax.ShapeDtypeStruct((RECV_MOST, wid...]
    unnamed x1 -> x0, local copies, waits for them, and re-layouts: 1.32 us -> none
    squeeze x1 -> x0, local copies, waits for them, and re-layouts: 1.14 us -> none  [per_device(): return (embedded, losses[0, :RECV_MOST])]
where the time goes in v3:
time: 59.2 us; the launch traced here: 59 us
  Pallas kernels  58.4 us (99%)
  between operations  0.64 us (1%)
    pallas_call x1, Pallas kernels, per_device(): pl.pallas_call(functools.partial(body, n_dp, n_mp), out_shape=(jax.ShapeD...  57.1 us
    pallas_call x1, Pallas kernels, per_device(): pl.pallas_call(hand_over, out_shape=(jax.ShapeDtypeStruct((RECV_MOST, wid...  1.33 us

profile of v3, /device:TPU:1, one launch (start us, length us, event | category | flops | bytes accessed | tf_op | source)
XLA Modules:
  0.0 59.0 jit_solution(17919090716963950807)
XLA Ops:
  0.6 57.1 %learner.1 = (f32[4,1024]{1,0:T(4,128)}, f32[1,128]{1,0:T(1,128)}) custom-call(s32[16]{0:T(128)} %selection_h.1, s32[16]{0:T(128)} %destination_h.1, f32[2]{0:T(128)} %loss_params_h.1, bf16[16,64,768]{2,1,0:T(8,128)(2,1)} %pixels.1, bf16[768,1024]{1,0:T(8,128)(2,1)} %patch_weight.1, bf16[2,4,8,1024]{3,2,1,0:T(8,128)(2,1)} %bitcast.3, ...), custom_call_target="tpu_custom_call" | custom-call | tf_op jit(solution)/shard_map/learner/pallas_call | solution.py:521
  57.7 1.3 %hand_over.1 = (f32[4,1024]{1,0:T(4,128)}, f32[4]{0:T(128)}) custom-call(f32[4,1024]{1,0:T(4,128)} %get-tuple-element.4.embedded, f32[1,128]{1,0:T(1,128)} %get-tuple-element.5.losses), custom_call_target="tpu_custom_call" | custom-call | tf_op jit(solution)/shard_map/hand_over/pallas_call | solution.py:538

commit v4 on v3

--- a/solution.py
+++ b/solution.py
@@ -172,9 +172,15 @@
         arrival(second, receives.at[2])
         send(second, sends.at[5], receives.at[5], to_left)
 
-    def ring_finish(from_left, from_right, far, receives):
+    def ring_near(from_left, from_right, receives):
         arrival(halves(from_left)[1], receives.at[1])
         arrival(halves(from_right)[0], receives.at[3])
+
+    def ring_finish(from_left, from_right, far, receives):
+        ring_near(from_left, from_right, receives)
+        ring_far(far, receives)
+
+    def ring_far(far, receives):
         arrival(halves(far)[0], receives.at[4])
         arrival(halves(far)[1], receives.at[5])
 
@@ -273,7 +279,7 @@
             normed[span, :] = norm_rows(hid[k, span, :], gain).astype(BF16)
             return carry
 
-        lax.fori_loop(0, rows // chunk_rows, one, 0, unroll=2)
+        lax.fori_loop(0, rows // chunk_rows, one, 0, unroll=4)
 
     half_lane = lax.broadcasted_iota(jnp.int32, (rows, 128), 1) < HEAD_DIM
     ones = jnp.ones((rows, 128), BF16)
@@ -302,9 +308,9 @@
         qkv[0] = (dot(normed[...], qkv_v[0]).astype(BF16) * BF16(HEAD_DIM ** (-0.5))).astype(BF16)
         qkv[1] = dot(normed[...], qkv_v[1]).astype(BF16)
         qkv[2] = dot(normed[...], qkv_v[2]).astype(BF16)
-        @pl.when(k == 2)
+        @pl.when(k == 0)
         def _():
-            caps_core()
+            pix_forward(2)
 
         for pair in range(qkv.shape[2] // 128):
             span = slice(pair * 128, pair * 128 + 128)
@@ -324,7 +330,6 @@
 
         @pl.when(k == 0)
         def _():
-            pix_forward(2)
             told(4)
             caps_z()
 
@@ -337,7 +342,50 @@
     lax.fori_loop(0, SEND_MOST, attend, 0)
     ctx_forward(1)
     wo_core()
-
+    caps_core()
+
+    for source, n in mp_sources:
+        arrival(wo.at[source, 1 - core], wc_r.at[n])
+    loads[10].wait()
+
+    def expand(k, carry):
+        ring_near(ctx.at[k, left], ctx.at[k, right], ctx_r.at[k])
+        context = jnp.concatenate([ctx[k, source] for source in (mp, left, right)], axis=1)
+        weights = jnp.concatenate([wo[source].reshape(-1, width) for source in (mp, left, right)], axis=0)
+        hid[k] = hid[k] + dot(context, weights)
+        ring_far(ctx.at[k, opposite], ctx_r.at[k])
+        hid[k] = hid[k] + dot(ctx[k, opposite], wo[opposite].reshape(-1, width))
+        norm_into(k, gain1)
+        own = jnp.sum(hid[k, pl.ds(pl.multiple_of(mp * patch_rows, patch_rows), patch_rows), :], axis=0, keepdims=True)
+        shared[mp, k] = diagonal(jnp.broadcast_to(own, (8, width)))
+        block = 512
+        for n in range(up_v.shape[1] // block):
+            span = slice(n * block, n * block + block)
+            units = jax.nn.gelu(dot(normed[...], up_v[:, span]))
+            total = jnp.sum(units, axis=0, keepdims=True)
+            summed[k, :, span] = jnp.broadcast_to(total, (8, block))
+
+        @pl.when(k == 0)
+        def _():
+            ctx_forward(2)
+
+        return carry
+
+    lax.fori_loop(0, SEND_MOST, expand, 0)
+
+    loads[11].wait()
+    totals = summed[...].reshape(SEND_MOST * 8, width)
+    high = totals.astype(BF16)
+    low = (totals - high.astype(F32)).astype(BF16)
+    down = dot(jnp.concatenate([high, low], axis=0), down_v[...])
+    down = down[: SEND_MOST * 8] + down[SEND_MOST * 8 :]
+    shared[mp] = shared[mp] + diagonal(down).reshape(SEND_MOST, 8, 128)
+
+    def share():
+        for other, n in mp_peers:
+            send(shared.at[mp], ar_s.at[n], ar_r.at[n], (dp, other))
+
+    share()
     arrival(caps.at[1 - core], cc_r)
     caps_all = caps[...].reshape(n_dp, SEND_MOST + 1, 8, 128)
     flat = n_dp * 8
@@ -369,46 +417,6 @@
         alive = jnp.max(jnp.where(lane == k, goals, -1.0), axis=1, keepdims=True)
         alive = jnp.max(jnp.broadcast_to(alive, (flat, 128)).reshape(n_dp, 8, 128), axis=1)
         sign_of[k] = jnp.where(alive >= 0.0, 1.0 - 2.0 * same, 0.0)
-
-    for source, n in mp_sources:
-        arrival(wo.at[source, 1 - core], wc_r.at[n])
-    loads[10].wait()
-
-    def expand(k, carry):
-        ring_finish(ctx.at[k, left], ctx.at[k, right], ctx.at[k, opposite], ctx_r.at[k])
-        context = jnp.concatenate([ctx[k, source] for source in range(n_mp)], axis=1)
-        hid[k] = hid[k] + dot(context, wo[...].reshape(width, width))
-        norm_into(k, gain1)
-        own = jnp.sum(hid[k, pl.ds(pl.multiple_of(mp * patch_rows, patch_rows), patch_rows), :], axis=0, keepdims=True)
-        shared[mp, k] = diagonal(jnp.broadcast_to(own, (8, width)))
-        block = 256
-        for n in range(up_v.shape[1] // block):
-            span = slice(n * block, n * block + block)
-            units = jax.nn.gelu(dot(normed[...], up_v[:, span]))
-            total = jnp.sum(units, axis=0, keepdims=True)
-            summed[k, :, span] = jnp.broadcast_to(total, (8, block))
-
-        @pl.when(k == 0)
-        def _():
-            ctx_forward(2)
-
-        return carry
-
-    lax.fori_loop(0, SEND_MOST, expand, 0)
-
-    loads[11].wait()
-    totals = summed[...].reshape(SEND_MOST * 8, width)
-    high = totals.astype(BF16)
-    low = (totals - high.astype(F32)).astype(BF16)
-    down = dot(jnp.concatenate([high, low], axis=0), down_v[...])
-    down = down[: SEND_MOST * 8] + down[SEND_MOST * 8 :]
-    shared[mp] = shared[mp] + diagonal(down).reshape(SEND_MOST, 8, 128)
-
-    def share():
-        for other, n in mp_peers:
-            send(shared.at[mp], ar_s.at[n], ar_r.at[n], (dp, other))
-
-    share()
     for source, n in mp_sources:
         arrival(shared.at[source], ar_r.at[n])
     pooled = (shared[0] + shared[1]) + (shared[2] + shared[3])

time: 59.2 us -> 56.9 us (0.961)
  Pallas kernels: 58.4 us -> 56.1 us
    pallas_call x1, Pallas kernels: 57.1 us -> 54.8 us  [per_device(): pl.pallas_call(functools.partial(body, n_dp, n_mp), out_shape=(jax.ShapeD...]
where the time goes in v4:
time: 56.9 us; the launch traced here: 56.8 us
  Pallas kernels  56.1 us (99%)
  between operations  0.64 us (1%)
    pallas_call x1, Pallas kernels, per_device(): pl.pallas_call(functools.partial(body, n_dp, n_mp), out_shape=(jax.ShapeD...  54.8 us
    pallas_call x1, Pallas kernels, per_device(): pl.pallas_call(hand_over, out_shape=(jax.ShapeDtypeStruct((RECV_MOST, wid...  1.33 us

profile of v4, /device:TPU:1, one launch (start us, length us, event | category | flops | bytes accessed | tf_op | source)
XLA Modules:
  0.0 56.8 jit_solution(5187053063462757598)
XLA Ops:
  0.6 54.8 %learner.1 = (f32[4,1024]{1,0:T(4,128)}, f32[1,128]{1,0:T(1,128)}) custom-call(s32[16]{0:T(128)} %selection_h.1, s32[16]{0:T(128)} %destination_h.1, f32[2]{0:T(128)} %loss_params_h.1, bf16[16,64,768]{2,1,0:T(8,128)(2,1)} %pixels.1, bf16[768,1024]{1,0:T(8,128)(2,1)} %patch_weight.1, bf16[2,4,8,1024]{3,2,1,0:T(8,128)(2,1)} %bitcast.3, ...), custom_call_target="tpu_custom_call" | custom-call | tf_op jit(solution)/shard_map/learner/pallas_call | solution.py:529
  55.4 1.3 %hand_over.1 = (f32[4,1024]{1,0:T(4,128)}, f32[4]{0:T(128)}) custom-call(f32[4,1024]{1,0:T(4,128)} %get-tuple-element.4.embedded, f32[1,128]{1,0:T(1,128)} %get-tuple-element.5.losses), custom_call_target="tpu_custom_call" | custom-call | tf_op jit(solution)/shard_map/hand_over/pallas_call | solution.py:546

commit v5 on v4

--- a/solution.py
+++ b/solution.py
@@ -90,7 +90,7 @@
             act(dp, n_dp // 2 + step)
             return carry
 
-        lax.fori_loop(1, n_dp // 2, both, 0)
+        lax.fori_loop(1, n_dp // 2, both, 0, unroll=True)
 
     loads = [
         (selection_h, selection), (destination_h, destination), (pixels, pixels_v), (captions, captions_v),
@@ -258,13 +258,13 @@
     tell(1)
     pix_forward(0)
     wo_x_forward()
-    pix_send(2)
     told(1)
     tell(2)
     place_core()
     told(2)
     tell(3)
     pix_forward(1)
+    pix_send(2)
     loads[6].wait()
     loads[7].wait()
     loads[8].wait()

time: 56.9 us -> 57 us (level)
  no operation moved by 1% of the time
where the time goes in v5:
time: 57 us; the launch traced here: 56.9 us
  Pallas kernels  56.2 us (99%)
  between operations  0.64 us (1%)
    pallas_call x1, Pallas kernels, per_device(): pl.pallas_call(functools.partial(body, n_dp, n_mp), out_shape=(jax.ShapeD...  54.9 us
    pallas_call x1, Pallas kernels, per_device(): pl.pallas_call(hand_over, out_shape=(jax.ShapeDtypeStruct((RECV_MOST, wid...  1.33 us

profile of v5, /device:TPU:1, one launch (start us, length us, event | category | flops | bytes accessed | tf_op | source)
XLA Modules:
  0.0 56.9 jit_solution(16909588013489789190)
XLA Ops:
  0.6 54.9 %learner.1 = (f32[4,1024]{1,0:T(4,128)}, f32[1,128]{1,0:T(1,128)}) custom-call(s32[16]{0:T(128)} %selection_h.1, s32[16]{0:T(128)} %destination_h.1, f32[2]{0:T(128)} %loss_params_h.1, bf16[16,64,768]{2,1,0:T(8,128)(2,1)} %pixels.1, bf16[768,1024]{1,0:T(8,128)(2,1)} %patch_weight.1, bf16[2,4,8,1024]{3,2,1,0:T(8,128)(2,1)} %bitcast.3, ...), custom_call_target="tpu_custom_call" | custom-call | tf_op jit(solution)/shard_map/learner/pallas_call | solution.py:529
  55.5 1.3 %hand_over.1 = (f32[4,1024]{1,0:T(4,128)}, f32[4]{0:T(128)}) custom-call(f32[4,1024]{1,0:T(4,128)} %get-tuple-element.4.embedded, f32[1,128]{1,0:T(1,128)} %get-tuple-element.5.losses), custom_call_target="tpu_custom_call" | custom-call | tf_op jit(solution)/shard_map/hand_over/pallas_call | solution.py:546
